TPU v7x, 32 devices: a whole 2x2x4 slice. The times are simulated.
32 devices in a mesh: ep: 8 (over y, x, core), fs: 4 (over z).
Axes of the slice: x: 2, y: 2, z: 4, core: 2. Of those that a mesh axis runs over, the one named last changes fastest.
Arguments:
- tokens: bfloat16 [6144, 2048], P(('ep', 'fs')), may hold values from -6 to 6
- attn_gain: bfloat16 [2048], P('fs'), may hold values from 0.5 to 1.5
- w_query: bfloat16 [2048, 2048], P('fs'), may hold values from -0.125 to 0.125
- w_key: bfloat16 [2048, 2048], P('fs'), may hold values from -0.125 to 0.125
- w_value: bfloat16 [2048, 2048], P('fs'), may hold values from -0.125 to 0.125
- query_gain: bfloat16 [128], P('fs'), may hold values from 0.5 to 1.5
- key_gain: bfloat16 [128], P('fs'), may hold values from 0.5 to 1.5
- w_output: bfloat16 [2048, 2048], P('fs'), may hold values from -2 to 2
- ffn_gain: bfloat16 [2048], P('fs'), may hold values from 0.5 to 1.5
- w_router: bfloat16 [2048, 32], P('fs'), may hold values from -0.0625 to 0.0625
- w_gate: bfloat16 [32, 2048, 1024], P('ep', 'fs'), may hold values from -0.125 to 0.125
- w_up: bfloat16 [32, 2048, 1024], P('ep', 'fs'), may hold values from -0.125 to 0.125
- w_down: bfloat16 [32, 1024, 2048], P('ep', 'fs'), may hold values from -0.5 to 0.5
- seq_lengths: int32 [8, 3], P('ep'), may hold values from 48 to 576, as said below
- span_places: int32 [8, 24], P('ep'), may hold values from 0 to 23, each once within a row
- routes: int32 [6144, 8], P(('ep', 'fs')), may hold values from 0 to 31, all different within a row; in each aligned block of 192 rows (0 to 191, 192 to 383, ...) at most 64 rows name the same one
- out_grad: bfloat16 [6144, 2048], P(('ep', 'fs')), may hold values from -6 to 6
Outputs:
- output: bfloat16 [6144, 2048], P(('ep', 'fs'))
- tokens_grad: bfloat16 [6144, 2048], P(('ep', 'fs'))
- attn_gain_grad: float32 [2048], P(('ep', 'fs'))
- w_query_grad: float32 [2048, 2048], P(('ep', 'fs'))
- w_key_grad: float32 [2048, 2048], P(('ep', 'fs'))
- w_value_grad: float32 [2048, 2048], P(('ep', 'fs'))
- query_gain_grad: float32 [128], P(('ep', 'fs'))
- key_gain_grad: float32 [128], P(('ep', 'fs'))
- w_output_grad: float32 [2048, 2048], P(('ep', 'fs'))
- ffn_gain_grad: float32 [2048], P(('ep', 'fs'))
- w_router_grad: float32 [2048, 32], P(('ep', 'fs'))
- w_gate_grad: float32 [32, 2048, 1024], P('ep', 'fs')
- w_up_grad: float32 [32, 2048, 1024], P('ep', 'fs')
- w_down_grad: float32 [32, 1024, 2048], P('ep', 'fs')
Inputs may be any that keep to these rules, and one draw needn't show every extreme that they name: `seq_lengths`: in each group the 3 lengths sum to 768; the longest is exactly 576. `span_places`: each row is a permutation of the group's span places. `routes`: each row names 8 distinct experts; among the rows of one device no expert is named more than 64 times, and in some device some expert exactly 64 times.
All inputs are finite; a program needn't handle non-finite values.
Results may differ from a plain program's by a relative error of at most 0.025.
Values may be sent and summed in bfloat16 or wider, within the bound.
A program may use at most 384 MiB of HBM per device.

v0:
```python
import math

import jax
import jax.numpy as jnp
from jax import lax
from jax.sharding import PartitionSpec as P

epsilon = 1e-06
rope_base = 10000.0
masked_score = -1000000000.0


def rms_scale(values):
    return lax.rsqrt(jnp.mean(values * values, axis=-1, keepdims=True) + epsilon)


def rope_tables(position, half_dim, head_dim):
    inverse = jnp.exp(
        jnp.arange(half_dim).astype(jnp.float32) * (-2.0 * math.log(rope_base) / head_dim)
    )
    angles = position.astype(jnp.float32)[:, None] * inverse[None, :]
    return (jnp.cos(angles), jnp.sin(angles))


def rotate(values, cosines, sines):
    half_dim = values.shape[-1] // 2
    former = values[..., :half_dim]
    latter = values[..., half_dim:]
    return jnp.concatenate(
        [former * cosines - latter * sines, latter * cosines + former * sines], axis=-1
    )


def rotate_back(grads, cosines, sines):
    half_dim = grads.shape[-1] // 2
    former = grads[..., :half_dim]
    latter = grads[..., half_dim:]
    return jnp.concatenate(
        [former * cosines + latter * sines, latter * cosines - former * sines], axis=-1
    )


def norm_back(values, scale, gain, upstream):
    weighted = upstream * gain
    inner_mean = jnp.mean(weighted * values, axis=-1, keepdims=True)
    return (
        scale * weighted - values * (scale * scale * scale) * inner_mean,
        upstream * values * scale,
    )


def rounded(values):
    return lax.optimization_barrier(values.astype(jnp.bfloat16)).astype(jnp.float32)


def group_layout(lengths_row, places_row, group_rows, span_rows):
    arrival = jnp.arange(group_rows, dtype=jnp.int32)
    span_hit = (arrival // span_rows)[:, None] == jnp.arange(places_row.shape[0], dtype=jnp.int32)[
        None, :
    ]
    places = (
        jnp.sum(jnp.where(span_hit, places_row[None, :], 0), axis=1) * span_rows
        + arrival % span_rows
    )
    seq_ends = jnp.cumsum(lengths_row)
    segment = jnp.sum((places[:, None] >= seq_ends[None, :]).astype(jnp.int32), axis=1)
    seq_starts = seq_ends - lengths_row
    picked = segment[:, None] == jnp.arange(lengths_row.shape[0], dtype=jnp.int32)[None, :]
    position = places - jnp.sum(jnp.where(picked, seq_starts[None, :], 0), axis=1)
    return (segment, position)


def on_device(
    tokens,
    attn_gain,
    w_query,
    w_key,
    w_value,
    query_gain,
    key_gain,
    w_output,
    ffn_gain,
    w_router,
    w_gate,
    w_up,
    w_down,
    seq_lengths,
    span_places,
    routes,
    out_grad,
):
    rows_dev, width = tokens.shape
    gathered = (
        lax.all_gather(attn_gain, "fs", axis=0, tiled=True),
        lax.all_gather(w_query, "fs", axis=0, tiled=True),
        lax.all_gather(w_key, "fs", axis=0, tiled=True),
        lax.all_gather(w_value, "fs", axis=0, tiled=True),
        lax.all_gather(query_gain, "fs", axis=0, tiled=True),
        lax.all_gather(key_gain, "fs", axis=0, tiled=True),
        lax.all_gather(w_output, "fs", axis=0, tiled=True),
        lax.all_gather(ffn_gain, "fs", axis=0, tiled=True),
        lax.all_gather(w_router, "fs", axis=0, tiled=True),
    )
    gain_one = gathered[0].astype(jnp.float32)
    query_full = gathered[1]
    key_full = gathered[2]
    value_full = gathered[3]
    gain_query = gathered[4].astype(jnp.float32)
    gain_key = gathered[5].astype(jnp.float32)
    output_full = gathered[6]
    gain_two = gathered[7].astype(jnp.float32)
    router_full = gathered[8]
    head_dim = gain_query.shape[0]
    heads_count = width // head_dim
    half_dim = head_dim // 2
    shard_count = lax.axis_size("fs")
    group_rows = rows_dev * shard_count
    span_rows = group_rows // span_places.shape[1]
    my_shard = lax.axis_index("fs")
    segment_all, position_all = group_layout(seq_lengths[0], span_places[0], group_rows, span_rows)
    segment_own = lax.dynamic_slice_in_dim(segment_all, my_shard * rows_dev, rows_dev)
    position_own = lax.dynamic_slice_in_dim(position_all, my_shard * rows_dev, rows_dev)
    cosines, sines = rope_tables(position_own, half_dim, head_dim)
    cosines = cosines[:, None, :]
    sines = sines[:, None, :]
    factor = 1.0 / math.sqrt(head_dim)
    hidden_in = tokens.astype(jnp.float32)
    scale_one = rms_scale(hidden_in)
    normed_one = (hidden_in * scale_one * gain_one).astype(jnp.bfloat16)
    query_pre = jnp.dot(normed_one, query_full, preferred_element_type=jnp.float32).reshape(
        rows_dev, heads_count, head_dim
    )
    key_pre = jnp.dot(normed_one, key_full, preferred_element_type=jnp.float32).reshape(
        rows_dev, heads_count, head_dim
    )
    value_low = jnp.dot(normed_one, value_full, preferred_element_type=jnp.float32).astype(
        jnp.bfloat16
    )
    query_scale = rms_scale(query_pre)
    key_scale = rms_scale(key_pre)
    query_rot = rotate(query_pre * query_scale * gain_query, cosines, sines).astype(jnp.bfloat16)
    key_rot = (
        rotate(key_pre * key_scale * gain_key, cosines, sines)
        .astype(jnp.bfloat16)
        .reshape(rows_dev, width)
    )

    def scores(key_piece):
        key_count = key_piece.shape[0]
        raw_scores = (
            jnp.einsum(
                "thd,phd->htp",
                query_rot,
                key_piece.reshape(key_count, heads_count, head_dim),
                preferred_element_type=jnp.float32,
            )
            * factor
        )
        allowed = segment_own[:, None] == segment_all[None, :]
        return jnp.where(allowed[None], raw_scores, masked_score)

    def sweep(step_fn, initial):
        return step_fn(
            initial,
            (
                lax.all_gather(key_rot, "fs", axis=0, tiled=True),
                lax.all_gather(value_low, "fs", axis=0, tiled=True),
            ),
            jnp.int32(0),
        )

    def stats_step(state_in, key_block, first_row):
        running_max, running_sum = state_in
        logits = scores(key_block[0])
        new_max = jnp.maximum(running_max, jnp.max(logits, axis=2))
        new_sum = jnp.sum(jnp.exp(logits - new_max[:, :, None]), axis=2)
        return (new_max, new_sum)

    stats = sweep(
        stats_step,
        (
            jnp.full((heads_count, rows_dev), -1e30, jnp.float32),
            jnp.zeros((heads_count, rows_dev), jnp.float32),
        ),
    )
    log_total = stats[0] + jnp.log(stats[1])

    def output_step(partial_sum, key_block, first_row):
        weights = jnp.exp(scores(key_block[0]) - log_total[:, :, None]).astype(jnp.bfloat16)
        value_rows = key_block[1].reshape(key_block[1].shape[0], heads_count, head_dim)
        return jnp.einsum("htp,phd->thd", weights, value_rows, preferred_element_type=jnp.float32)

    attended = sweep(output_step, jnp.zeros((rows_dev, heads_count, head_dim), jnp.float32))
    attended_low = attended.reshape(rows_dev, width).astype(jnp.bfloat16)
    hidden_mid = hidden_in + jnp.dot(attended_low, output_full, preferred_element_type=jnp.float32)
    scale_two = rms_scale(hidden_mid)
    normed_two = (hidden_mid * scale_two * gain_two).astype(jnp.bfloat16)
    logits_all = jnp.dot(normed_two, router_full, preferred_element_type=jnp.float32)
    experts_total = router_full.shape[1]
    top_count = routes.shape[1]
    ep_count = lax.axis_size("ep")
    local_experts = experts_total // ep_count
    capacity = 4 * rows_dev * top_count // (3 * experts_total)
    route_hit = routes[:, :, None] == jnp.arange(experts_total, dtype=jnp.int32)[None, None, :]
    chosen = jnp.sum(jnp.where(route_hit, logits_all[:, None, :], 0.0), axis=2)
    chosen_peak = jnp.max(chosen, axis=1, keepdims=True)
    chosen_exp = jnp.exp(chosen - chosen_peak)
    gates = chosen_exp / jnp.sum(chosen_exp, axis=1, keepdims=True)
    pair_count = rows_dev * top_count
    flat_routes = routes.reshape(pair_count)
    matches = (flat_routes[:, None] == jnp.arange(experts_total, dtype=jnp.int32)[None, :]).astype(
        jnp.int32
    )
    slot_rank = jnp.sum((jnp.cumsum(matches, axis=0) - 1) * matches, axis=1)
    slot_index = flat_routes * capacity + slot_rank
    slot_owner = (
        jnp.full((experts_total * capacity,), pair_count, jnp.int32)
        .at[slot_index]
        .set(jnp.arange(pair_count, dtype=jnp.int32))
    )
    slot_live = slot_owner < pair_count
    owner_pair = jnp.where(slot_live, slot_owner, 0)
    source_rows = owner_pair // top_count
    send_rows = jnp.where(
        slot_live[:, None], normed_two[source_rows], jnp.zeros((), jnp.bfloat16)
    ).reshape(ep_count, local_experts, capacity, width)
    expert_gate, expert_up, expert_down = (
        lax.all_gather(w_gate, "fs", axis=1, tiled=True),
        lax.all_gather(w_up, "fs", axis=1, tiled=True),
        lax.all_gather(w_down, "fs", axis=1, tiled=True),
    )
    received_rows = lax.all_to_all(send_rows, "ep", split_axis=0, concat_axis=0, tiled=True)
    gate_value = jnp.einsum(
        "secd,edf->secf", received_rows, expert_gate, preferred_element_type=jnp.float32
    )
    up_value = jnp.einsum(
        "secd,edf->secf", received_rows, expert_up, preferred_element_type=jnp.float32
    )
    activated = (jax.nn.silu(gate_value) * up_value).astype(jnp.bfloat16)
    result = jnp.einsum(
        "secf,efd->secd", activated, expert_down, preferred_element_type=jnp.float32
    ).astype(jnp.bfloat16)
    returned = lax.all_to_all(result, "ep", split_axis=0, concat_axis=0, tiled=True)
    returned_pairs = (
        returned.reshape(experts_total * capacity, width)[slot_index]
        .astype(jnp.float32)
        .reshape(rows_dev, top_count, width)
    )
    mixed = jnp.sum(gates[:, :, None] * returned_pairs, axis=1)
    output = (hidden_mid + mixed).astype(jnp.bfloat16)
    grad_out = out_grad.astype(jnp.float32)
    grad_gates = jnp.sum(grad_out[:, None, :] * returned_pairs, axis=2)
    grad_chosen = gates * (grad_gates - jnp.sum(gates * grad_gates, axis=1, keepdims=True))
    grad_logits = jnp.sum(jnp.where(route_hit, grad_chosen[:, :, None], 0.0), axis=1).astype(
        jnp.bfloat16
    )
    grad_pairs = (
        (gates[:, :, None] * grad_out[:, None, :]).astype(jnp.bfloat16).reshape(pair_count, width)
    )
    grad_send = jnp.where(
        slot_live[:, None], grad_pairs[owner_pair], jnp.zeros((), jnp.bfloat16)
    ).reshape(ep_count, local_experts, capacity, width)
    grad_rows = lax.all_to_all(grad_send, "ep", split_axis=0, concat_axis=0, tiled=True)
    back_gate, back_up, back_down = (
        lax.all_gather(w_gate, "fs", axis=1, tiled=True),
        lax.all_gather(w_up, "fs", axis=1, tiled=True),
        lax.all_gather(w_down, "fs", axis=1, tiled=True),
    )
    activated_back = (jax.nn.silu(gate_value) * up_value).astype(jnp.bfloat16)
    grad_activated = jnp.einsum(
        "secd,efd->secf", grad_rows, back_down, preferred_element_type=jnp.float32
    )
    sigmoid_gate = jax.nn.sigmoid(gate_value)
    grad_up = (grad_activated * gate_value * sigmoid_gate).astype(jnp.bfloat16)
    grad_gate = (
        grad_activated * up_value * sigmoid_gate * (1.0 + gate_value * (1.0 - sigmoid_gate))
    ).astype(jnp.bfloat16)
    grad_received = (
        jnp.einsum("secf,edf->secd", grad_gate, back_gate, preferred_element_type=jnp.float32)
        + jnp.einsum("secf,edf->secd", grad_up, back_up, preferred_element_type=jnp.float32)
    ).astype(jnp.bfloat16)
    grad_back = lax.all_to_all(grad_received, "ep", split_axis=0, concat_axis=0, tiled=True)
    down_grad = jnp.einsum(
        "secf,secd->efd", activated_back, grad_rows, preferred_element_type=jnp.float32
    )
    gate_grad = jnp.einsum(
        "secd,secf->edf", received_rows, grad_gate, preferred_element_type=jnp.float32
    )
    up_grad = jnp.einsum(
        "secd,secf->edf", received_rows, grad_up, preferred_element_type=jnp.float32
    )
    expert_sums = (
        lax.psum_scatter(
            gate_grad.astype(jnp.bfloat16), "fs", scatter_dimension=1, tiled=True
        ).astype(jnp.float32),
        lax.psum_scatter(
            up_grad.astype(jnp.bfloat16), "fs", scatter_dimension=1, tiled=True
        ).astype(jnp.float32),
        lax.psum_scatter(
            down_grad.astype(jnp.bfloat16), "fs", scatter_dimension=1, tiled=True
        ).astype(jnp.float32),
    )
    grad_from_experts = jnp.sum(
        grad_back.reshape(experts_total * capacity, width)[slot_index]
        .astype(jnp.float32)
        .reshape(rows_dev, top_count, width),
        axis=1,
    )
    router_grad = jnp.einsum(
        "td,te->de", normed_two, grad_logits, preferred_element_type=jnp.float32
    )
    grad_normed_two = grad_from_experts + jnp.einsum(
        "te,de->td", grad_logits, router_full, preferred_element_type=jnp.float32
    )
    grad_mid_norm, gain_two_terms = norm_back(hidden_mid, scale_two, gain_two, grad_normed_two)
    gain_two_grad = jnp.sum(gain_two_terms, axis=0)
    grad_mid = grad_out + grad_mid_norm
    grad_branch = grad_mid.astype(jnp.bfloat16)
    output_w_grad = jnp.einsum(
        "ti,to->io", attended_low, grad_branch, preferred_element_type=jnp.float32
    )
    grad_attended = (
        jnp.einsum("to,io->ti", grad_branch, output_full, preferred_element_type=jnp.float32)
        .astype(jnp.bfloat16)
        .reshape(rows_dev, heads_count, head_dim)
    )

    def delta_step(partial_sum, key_block, first_row):
        weights = jnp.exp(scores(key_block[0]) - log_total[:, :, None])
        value_rows = key_block[1].reshape(key_block[1].shape[0], heads_count, head_dim)
        grad_weights = jnp.einsum(
            "thd,phd->htp", grad_attended, value_rows, preferred_element_type=jnp.float32
        )
        return jnp.sum(weights * grad_weights, axis=2)

    delta = sweep(delta_step, jnp.zeros((heads_count, rows_dev), jnp.float32))

    def gradient_step(state_in, key_block, first_row):
        key_count = key_block[0].shape[0]
        key_rows = key_block[0].reshape(key_count, heads_count, head_dim)
        value_rows = key_block[1].reshape(key_count, heads_count, head_dim)
        weights = jnp.exp(scores(key_block[0]) - log_total[:, :, None])
        grad_weights = jnp.einsum(
            "thd,phd->htp", grad_attended, value_rows, preferred_element_type=jnp.float32
        )
        grad_scores = (weights * (grad_weights - delta[:, :, None])).astype(jnp.bfloat16)
        grad_query = (
            jnp.einsum("htp,phd->thd", grad_scores, key_rows, preferred_element_type=jnp.float32)
            * factor
        )
        key_part = (
            jnp.einsum("htp,thd->phd", grad_scores, query_rot, preferred_element_type=jnp.float32)
            * factor
        ).reshape(key_count, width)
        value_part = jnp.einsum(
            "htp,thd->phd",
            weights.astype(jnp.bfloat16),
            grad_attended,
            preferred_element_type=jnp.float32,
        ).reshape(key_count, width)
        return (grad_query, key_part, value_part)

    grad_query, key_grads, value_grads = sweep(
        gradient_step,
        (
            jnp.zeros((rows_dev, heads_count, head_dim), jnp.float32),
            jnp.zeros((group_rows, width), jnp.float32),
            jnp.zeros((group_rows, width), jnp.float32),
        ),
    )
    grad_key_own, grad_value_own = (
        lax.psum_scatter(
            key_grads.astype(jnp.bfloat16), "fs", scatter_dimension=0, tiled=True
        ).astype(jnp.float32),
        lax.psum_scatter(
            value_grads.astype(jnp.bfloat16), "fs", scatter_dimension=0, tiled=True
        ).astype(jnp.float32),
    )
    grad_query_norm = rotate_back(rounded(grad_query), cosines, sines)
    grad_query_pre, query_gain_terms = norm_back(
        query_pre, query_scale, gain_query, grad_query_norm
    )
    grad_key_norm = rotate_back(
        rounded(grad_key_own.reshape(rows_dev, heads_count, head_dim)), cosines, sines
    )
    grad_key_pre, key_gain_terms = norm_back(key_pre, key_scale, gain_key, grad_key_norm)
    query_gain_grad = jnp.sum(query_gain_terms, axis=(0, 1))
    key_gain_grad = jnp.sum(key_gain_terms, axis=(0, 1))
    grad_query_low = grad_query_pre.reshape(rows_dev, width).astype(jnp.bfloat16)
    grad_key_low = grad_key_pre.reshape(rows_dev, width).astype(jnp.bfloat16)
    grad_value_low = grad_value_own.astype(jnp.bfloat16)
    query_w_grad = jnp.einsum(
        "ti,to->io", normed_one, grad_query_low, preferred_element_type=jnp.float32
    )
    key_w_grad = jnp.einsum(
        "ti,to->io", normed_one, grad_key_low, preferred_element_type=jnp.float32
    )
    value_w_grad = jnp.einsum(
        "ti,to->io", normed_one, grad_value_low, preferred_element_type=jnp.float32
    )
    grad_normed_one = jnp.einsum(
        "to,io->ti", grad_query_low, query_full, preferred_element_type=jnp.float32
    )
    grad_normed_one = grad_normed_one + jnp.einsum(
        "to,io->ti", grad_key_low, key_full, preferred_element_type=jnp.float32
    )
    grad_normed_one = grad_normed_one + jnp.einsum(
        "to,io->ti", grad_value_low, value_full, preferred_element_type=jnp.float32
    )
    grad_in_norm, gain_one_terms = norm_back(hidden_in, scale_one, gain_one, grad_normed_one)
    gain_one_grad = jnp.sum(gain_one_terms, axis=0)
    tokens_grad = (grad_mid + grad_in_norm).astype(jnp.bfloat16)
    layer_sums = (
        lax.psum_scatter(gain_one_grad, ("ep", "fs"), scatter_dimension=0, tiled=True),
        lax.psum_scatter(query_w_grad, ("ep", "fs"), scatter_dimension=0, tiled=True),
        lax.psum_scatter(key_w_grad, ("ep", "fs"), scatter_dimension=0, tiled=True),
        lax.psum_scatter(value_w_grad, ("ep", "fs"), scatter_dimension=0, tiled=True),
        lax.psum_scatter(query_gain_grad, ("ep", "fs"), scatter_dimension=0, tiled=True),
        lax.psum_scatter(key_gain_grad, ("ep", "fs"), scatter_dimension=0, tiled=True),
        lax.psum_scatter(output_w_grad, ("ep", "fs"), scatter_dimension=0, tiled=True),
        lax.psum_scatter(gain_two_grad, ("ep", "fs"), scatter_dimension=0, tiled=True),
        lax.psum_scatter(router_grad, ("ep", "fs"), scatter_dimension=0, tiled=True),
    )
    return (
        output,
        tokens_grad,
        layer_sums[0],
        layer_sums[1],
        layer_sums[2],
        layer_sums[3],
        layer_sums[4],
        layer_sums[5],
        layer_sums[6],
        layer_sums[7],
        layer_sums[8],
        expert_sums[0],
        expert_sums[1],
        expert_sums[2],
    )


def solution(mesh):
    return jax.shard_map(
        on_device,
        mesh=mesh,
        in_specs=(
            P(("ep", "fs"), None),
            P("fs"),
            P("fs", None),
            P("fs", None),
            P("fs", None),
            P("fs"),
            P("fs"),
            P("fs", None),
            P("fs"),
            P("fs", None),
            P("ep", "fs", None),
            P("ep", "fs", None),
            P("ep", "fs", None),
            P("ep", None),
            P("ep", None),
            P(("ep", "fs"), None),
            P(("ep", "fs"), None),
        ),
        out_specs=(
            P(("ep", "fs"), None),
            P(("ep", "fs"), None),
            P(("ep", "fs")),
            P(("ep", "fs"), None),
            P(("ep", "fs"), None),
            P(("ep", "fs"), None),
            P(("ep", "fs")),
            P(("ep", "fs")),
            P(("ep", "fs"), None),
            P(("ep", "fs")),
            P(("ep", "fs"), None),
            P("ep", "fs", None),
            P("ep", "fs", None),
            P("ep", "fs", None),
        ),
        check_vma=False,
    )
```

profile of v0, /device:TPU:0, one launch (start us, length us, event | category | flops | bytes accessed | tf_op | source)
XLA Modules:
  0.0 4459.5 jit_solution(14371337558782742955)
XLA Ops:
  9.5 13.6 all-gather
  25.0 11.0 all-reduce.7
  37.8 124.4 %all-gather.18.cloned.1.call-done = bf16[2048,2048]{1,0:T(8,128)(2,1)} async-done(((bf16[512,2048]{1,0:T(8,128)(2,1)}), bf16[2048,2048]{1,0:T(8,128)(2,1)}) %all-gather.18.cloned.1.call-update) | async-done | bytes 8388624 | tf_op jit(solution)/shard_map/all_gather | solution.py:96
  169.4 142.2 %all-gather.16.cloned.1.call-done = bf16[2048,2048]{1,0:T(8,128)(2,1)} async-done(((bf16[512,2048]{1,0:T(8,128)(2,1)}), bf16[2048,2048]{1,0:T(8,128)(2,1)}) %all-gather.16.cloned.1.call-update) | async-done | bytes 8388624 | tf_op jit(solution)/shard_map/all_gather | solution.py:95
  324.6 136.4 %all-gather.12.cloned.1.call-done = bf16[2048,2048]{1,0:T(8,128)(2,1)} async-done(((bf16[512,2048]{1,0:T(8,128)(2,1)}), bf16[2048,2048]{1,0:T(8,128)(2,1)}) %all-gather.12.cloned.1.call-update) | async-done | bytes 8388624 | tf_op jit(solution)/shard_map/all_gather | solution.py:97
  470.4 12.4 all-gather.1
  485.0 15.9 reduce-window.11
  512.4 15.1 all_gather.60
  540.8 49.8 %all-gather.14.cloned.1.call-done = bf16[768,2048]{1,0:T(8,128)(2,1)} async-done(((bf16[192,2048]{1,0:T(8,128)(2,1)}), bf16[768,2048]{1,0:T(8,128)(2,1)}) %all-gather.14.cloned.1.call-update) | async-done | bytes 3145744 | tf_op jit(solution)/shard_map/all_gather | solution.py:167
  598.2 142.1 %all-gather.22.cloned.1.call-done = bf16[2048,2048]{1,0:T(8,128)(2,1)} async-done(((bf16[512,2048]{1,0:T(8,128)(2,1)}), bf16[2048,2048]{1,0:T(8,128)(2,1)}) %all-gather.22.cloned.1.call-update) | async-done | bytes 8388624 | tf_op jit(solution)/shard_map/all_gather | solution.py:100
  748.2 10.9 gather_fusion
  762.6 20.1 gather_fusion.2
  782.7 9.2 broadcast_select_fusion
  791.9 97.5 %all_to_all.20 = bf16[8,4,64,2048]{3,2,1,0:T(8,128)(2,1)} all-to-all(bf16[8,4,64,2048]{3,2,1,0:T(8,128)(2,1)S(1)} %get-tuple-element.58), channel_id=1, replica_groups=mesh['ep'=8,'fs'=4] {'ep'}, dimensions={0} | all-to-all | bytes 16777216 | tf_op jit(solution)/shard_map/all_to_all | solution.py:232
  894.4 132.4 %all-gather.24.cloned.1.call-done = bf16[4,2048,1024]{2,1,0:T(8,128)(2,1)} async-done(((bf16[4,512,1024]{2,1,0:T(8,128)(2,1)}), bf16[4,2048,1024]{2,1,0:T(8,128)(2,1)}) %all-gather.24.cloned.1.call-update) | async-done | bytes 16777232 | tf_op jit(solution)/shard_map/all_gather | solution.py:228
  1026.8 16.8 fusion.6
  1043.6 269.7 %all-gather.26.cloned.1.call-done = bf16[4,2048,1024]{2,1,0:T(8,128)(2,1)} async-done(((bf16[4,512,1024]{2,1,0:T(8,128)(2,1)}), bf16[4,2048,1024]{2,1,0:T(8,128)(2,1)}) %all-gather.26.cloned.1.call-update) | async-done | bytes 16777232 | tf_op jit(solution)/shard_map/all_gather | solution.py:229
  1313.3 16.9 fusion.2
  1330.2 269.7 %all-gather.28.cloned.1.call-done = bf16[4,1024,2048]{2,1,0:T(8,128)(2,1)} async-done(((bf16[4,256,2048]{2,1,0:T(8,128)(2,1)}), bf16[4,1024,2048]{2,1,0:T(8,128)(2,1)}) %all-gather.28.cloned.1.call-update) | async-done | bytes 16777232 | tf_op jit(solution)/shard_map/all_gather | solution.py:230
  1599.9 22.8 fusion.18
  1622.7 17.7 convert_bitcast_fusion
  1640.4 8.4 copy.259
  1653.8 17.0 fusion
  1670.8 18.2 fusion.15
  1689.0 8.4 copy.262
  1697.4 50.4 %all-to-all-done.1 = bf16[8,4,64,2048]{3,2,1,0:T(8,128)(2,1)} async-done(((bf16[8,4,64,2048]{3,2,1,0:T(8,128)(2,1)}), bf16[8,4,64,2048]{3,2,1,0:T(8,128)(2,1)}, u32[]{:S(2)}, u32[]{:S(2)}) %all-to-all-start.1) | async-done | bytes 8388640 | tf_op jit(solution)/shard_map/all_to_all | solution.py:243
  1753.3 17.3 gather_fusion.1
  1770.6 7.7 fusion.13
  1778.4 68.8 %all-to-all-done.3 = bf16[8,4,64,2048]{3,2,1,0:T(8,128)(2,1)} async-done(((bf16[8,4,64,2048]{3,2,1,0:T(8,128)(2,1)}), bf16[8,4,64,2048]{3,2,1,0:T(8,128)(2,1)}, u32[]{:S(2)}, u32[]{:S(2)}) %all-to-all-start.3) | async-done | bytes 8388640 | tf_op jit(solution)/shard_map/all_to_all | solution.py:282
  1847.2 17.3 gather_fusion.3
  1864.6 8.0 convert_reduce_fusion
  1911.9 15.9 bitcast_convert_fusion.2
  1927.9 16.2 bitcast_convert_fusion.1
  1944.2 16.5 bitcast_convert_fusion
  1961.8 8.1 fusion.72
  1971.1 9.4 fusion.119
  1987.5 20.7 reduce-scatter.15.cloned.1.call-done
  2018.6 8.3 fusion.121
  2037.3 8.2 fusion.123
  2045.5 101.7 %reduce-scatter.33.cloned.1.call-done = f32[64,32]{1,0:T(8,128)} async-done(((f32[2048,32]{1,0:T(8,128)}), f32[64,32]{1,0:T(8,128)}) %reduce-scatter.33.cloned.1.call-update) | async-done | bytes 8208
  2166.3 39.7 all-reduce.6
  2211.1 216.6 %reduce-scatter.25.cloned.1.call-done = bf16[4,512,1024]{2,1,0:T(8,128)(2,1)} async-done(((bf16[4,2048,1024]{2,1,0:T(8,128)(2,1)}), bf16[4,512,1024]{2,1,0:T(8,128)(2,1)}) %reduce-scatter.25.cloned.1.call-update) | async-done | bytes 4194320 | tf_op jit(solution)/shard_map/reduce_scatter | solution.py:293
  2434.3 276.7 %reduce-scatter.27.cloned.1.call-done = bf16[4,512,1024]{2,1,0:T(8,128)(2,1)} async-done(((bf16[4,2048,1024]{2,1,0:T(8,128)(2,1)}), bf16[4,512,1024]{2,1,0:T(8,128)(2,1)}) %reduce-scatter.27.cloned.1.call-update) | async-done | bytes 4194320 | tf_op jit(solution)/shard_map/reduce_scatter | solution.py:296
  2717.6 276.7 %reduce-scatter.29.cloned.1.call-done = bf16[4,256,2048]{2,1,0:T(8,128)(2,1)} async-done(((bf16[4,1024,2048]{2,1,0:T(8,128)(2,1)}), bf16[4,256,2048]{2,1,0:T(8,128)(2,1)}) %reduce-scatter.29.cloned.1.call-update) | async-done | bytes 4194320 | tf_op jit(solution)/shard_map/reduce_scatter | solution.py:299
  3000.9 357.3 %reduce-scatter.23.cloned.1.call-done = f32[64,2048]{1,0:T(8,128)} async-done(((f32[2048,2048]{1,0:T(8,128)}), f32[64,2048]{1,0:T(8,128)}) %reduce-scatter.23.cloned.1.call-update) | async-done | bytes 524304 | tf_op jit(solution)/shard_map/reduce_scatter | solution.py:420
  3358.3 364.7 %reduce-scatter.21.cloned.1.call-done = f32[64,2048]{1,0:T(8,128)} async-done(((f32[2048,2048]{1,0:T(8,128)}), f32[64,2048]{1,0:T(8,128)}) %reduce-scatter.21.cloned.1.call-update) | async-done | bytes 524304 | tf_op jit(solution)/shard_map/reduce_scatter | solution.py:417
  3722.9 364.7 %reduce-scatter.19.cloned.1.call-done = f32[64,2048]{1,0:T(8,128)} async-done(((f32[2048,2048]{1,0:T(8,128)}), f32[64,2048]{1,0:T(8,128)}) %reduce-scatter.19.cloned.1.call-update) | async-done | bytes 524304 | tf_op jit(solution)/shard_map/reduce_scatter | solution.py:416
  4087.6 364.9 %reduce-scatter.17.cloned.1.call-done = f32[64,2048]{1,0:T(8,128)} async-done(((f32[2048,2048]{1,0:T(8,128)}), f32[64,2048]{1,0:T(8,128)}) %reduce-scatter.17.cloned.1.call-update) | async-done | bytes 524304 | tf_op jit(solution)/shard_map/reduce_scatter | solution.py:415
  (352 shorter events, 208.8 us)
Async XLA Ops:
  7.2 17.5 copy-start.76
  7.2 28.8 copy-start.77
  7.2 29.0 copy-start.74
  7.2 29.4 copy-start.3
  7.3 155.0 %all-gather.18.cloned.1.call-start = ((), (), s32[]{:S(2)}) async-start(), calls=%async_computation.17 | async-start | bytes 10485760 | tf_op jit(solution)/shard_map/all_gather | solution.py:96
  8.0 303.6 %all-gather.16.cloned.1.call-start = ((), (), s32[]{:S(2)}) async-start(), calls=%async_computation.16 | async-start | bytes 10485760 | tf_op jit(solution)/shard_map/all_gather | solution.py:95
  8.7 452.3 %all-gather.12.cloned.1.call-start = ((), (), s32[]{:S(2)}) async-start(), calls=%async_computation.14 | async-start | bytes 10485760 | tf_op jit(solution)/shard_map/all_gather | solution.py:97
  9.5 518.2 %all-gather.20.cloned.1.call-start = ((), (), s32[]{:S(2)}) async-start(), calls=%async_computation.18 | async-start | bytes 3932160 | tf_op jit(solution)/shard_map/all_gather | solution.py:166
  23.2 437.8 %copy-start.41 = (f32[4,1,512]{2,1,0:T(1,128)}, f32[4,1,512]{2,1,0:T(1,128)S(1)}, u32[]{:S(2)}) copy-start(f32[4,1,512]{2,1,0:T(1,128)S(1)} %convert_element_type.244) | copy-start | bytes 24580
  36.0 282.9 %copy-start.66 = (f32[128]{0:T(128)}, f32[128]{0:T(128)S(1)}, u32[]{:S(2)}) copy-start(f32[128]{0:T(128)S(1)} %convert_element_type.192) | copy-start | bytes 1540
  36.0 282.9 %copy-start.68 = (f32[128]{0:T(128)}, f32[128]{0:T(128)S(1)}, u32[]{:S(2)}) copy-start(f32[128]{0:T(128)S(1)} %convert_element_type.195) | copy-start | bytes 1540
  37.4 423.7 %copy-start.53 = (f32[192]{0:T(256)}, f32[192]{0:T(256)S(1)}, u32[]{:S(2)}) copy-start(f32[192]{0:T(256)S(1)} %get-tuple-element.62) | copy-start | bytes 2308
  37.8 283.4 %copy-start.33 = (f32[192,64]{1,0:T(8,128)}, f32[192,64]{1,0:T(8,128)S(1)}, u32[]{:S(2)}) copy-start(f32[192,64]{1,0:T(8,128)S(1)} %get-tuple-element.59) | copy-start | bytes 147460
  37.8 283.4 %copy-start.35 = (f32[192,64]{1,0:T(8,128)}, f32[192,64]{1,0:T(8,128)S(1)}, u32[]{:S(2)}) copy-start(f32[192,64]{1,0:T(8,128)S(1)} %get-tuple-element.60) | copy-start | bytes 147460
  323.2 209.1 %copy-start.17 = (bf16[192,16,64]{2,0,1:T(8,128)(2,1)}, bf16[192,16,64]{2,0,1:T(8,128)(2,1)S(1)}, u32[]{:S(2)}) copy-start(bf16[192,16,64]{2,0,1:T(8,128)(2,1)S(1)} %get-tuple-element.41) | copy-start | bytes 1179652
  324.5 266.0 %all-gather.14.cloned.1.call-start = ((), (), s32[]{:S(2)}) async-start(), calls=%async_computation.15 | async-start | bytes 3932160 | tf_op jit(solution)/shard_map/all_gather | solution.py:167
  467.2 273.1 %all-gather.22.cloned.1.call-start = ((), (), s32[]{:S(2)}) async-start(), calls=%async_computation.19 | async-start | bytes 10485760 | tf_op jit(solution)/shard_map/all_gather | solution.py:100
  467.7 559.0 %all-gather.24.cloned.1.call-start = ((), (), s32[]{:S(2)}) async-start(), calls=%async_computation.20 | async-start | bytes 20971520 | tf_op jit(solution)/shard_map/all_gather | solution.py:228
  468.5 844.8 %all-gather.26.cloned.1.call-start = ((), (), s32[]{:S(2)}) async-start(), calls=%async_computation.21 | async-start | bytes 20971520 | tf_op jit(solution)/shard_map/all_gather | solution.py:229
  469.3 1130.6 %all-gather.28.cloned.1.call-start = ((), (), s32[]{:S(2)}) async-start(), calls=%async_computation.22 | async-start | bytes 20971520 | tf_op jit(solution)/shard_map/all_gather | solution.py:230
  482.9 263.3 %copy-start.51 = (f32[4,1,512]{2,1,0:T(1,128)}, f32[4,1,512]{2,1,0:T(1,128)S(1)}, u32[]{:S(2)}) copy-start(f32[4,1,512]{2,1,0:T(1,128)S(1)} %convert_element_type.245) | copy-start | bytes 24580
  484.2 274.9 %copy-start.10 = (f32[192,2048]{1,0:T(8,128)}, f32[192,2048]{1,0:T(8,128)S(1)}, u32[]{:S(2)}) copy-start(f32[192,2048]{1,0:T(8,128)S(1)} %convert_element_type.210) | copy-start | bytes 4718596
  527.5 219.5 %copy-start.29 = (bf16[2048,32]{0,1:T(8,128)(2,1)}, bf16[2048,32]{0,1:T(8,128)(2,1)S(1)}, u32[]{:S(2)}) copy-start(bf16[2048,32]{0,1:T(8,128)(2,1)S(1)} %all_gather.60) | copy-start | bytes 393220
  527.6 62.9 %copy-start.23 = (pred[192,768]{1,0:T(8,128)(4,1)}, pred[192,768]{1,0:T(8,128)(4,1)S(1)}, u32[]{:S(2)}) copy-start(pred[192,768]{1,0:T(8,128)(4,1)S(1)} %broadcast_compare_fusion) | copy-start | bytes 442372
  540.7 57.4 %copy-start.43 = (f32[16,192]{1,0:T(8,128)}, f32[16,192]{1,0:T(8,128)S(1)}, u32[]{:S(2)}) copy-start(f32[16,192]{1,0:T(8,128)S(1)} %log_add_fusion) | copy-start | bytes 36868
  598.2 147.4 %copy-start.31 = (bf16[16,24,8,128]{3,2,1,0:T(8,128)(2,1)}, bf16[16,24,8,128]{3,2,1,0:T(8,128)(2,1)S(1)}, u32[]{:S(2)}) copy-start(bf16[16,24,8,128]{3,2,1,0:T(8,128)(2,1)S(1)} %fusion.67) | copy-start | bytes 2359300
  889.4 440.7 %all-to-all-start.2 = ((bf16[8,4,64,2048]{3,2,1,0:T(8,128)(2,1)}), bf16[8,4,64,2048]{3,2,1,0:T(8,128)(2,1)}, u32[]{:S(2)}, u32[]{:S(2)}) async-start(bf16[8,4,64,2048]{3,2,1,0:T(8,128)(2,1)} %get-tuple-element.57), calls=%async_computation.2 | async-start | bytes 16777216 | tf_op jit(solution)/shard_map/all_to_all | solution.py:263
  1648.8 99.0 %all-to-all-start.1 = ((bf16[8,4,64,2048]{3,2,1,0:T(8,128)(2,1)}), bf16[8,4,64,2048]{3,2,1,0:T(8,128)(2,1)}, u32[]{:S(2)}, u32[]{:S(2)}) async-start(bf16[8,4,64,2048]{3,2,1,0:T(8,128)(2,1)} %copy.259), calls=%async_computation.1 | async-start | bytes 16777216 | tf_op jit(solution)/shard_map/all_to_all | solution.py:243
  1697.4 55.8 %copy-start.59 = (s32[1536]{0:T(1024)S(1)}, s32[1536]{0:T(1024)}, u32[]{:S(2)}) copy-start(s32[1536]{0:T(1024)} %copy-done.58) | copy-start | bytes 18436
  1747.9 99.4 %all-to-all-start.3 = ((bf16[8,4,64,2048]{3,2,1,0:T(8,128)(2,1)}), bf16[8,4,64,2048]{3,2,1,0:T(8,128)(2,1)}, u32[]{:S(2)}, u32[]{:S(2)}) async-start(bf16[8,4,64,2048]{3,2,1,0:T(8,128)(2,1)} %copy.262), calls=%async_computation.3 | async-start | bytes 16777216 | tf_op jit(solution)/shard_map/all_to_all | solution.py:282
  1753.2 217.0 %reduce-scatter.31.cloned.1.call-start = ((), (), s32[]{:S(2)}) async-start(), calls=%async_computation.31 | async-start | bytes 3932160
  1753.3 17.3 copy-start.11
  1753.3 17.3 copy-start.38
  1875.7 85.1 %copy-start.15 = (f32[192,2048]{1,0:T(8,128)}, f32[192,2048]{1,0:T(8,128)S(1)}, u32[]{:S(2)}) copy-start(f32[192,2048]{1,0:T(8,128)S(1)} %get-tuple-element.45) | copy-start | bytes 4718596
  1888.0 120.2 %reduce-scatter.15.cloned.1.call-start = ((), (), s32[]{:S(2)}) async-start(), calls=%async_computation.23 | async-start | bytes 3932160 | tf_op jit(solution)/shard_map/reduce_scatter | solution.py:372
  1909.2 238.0 %reduce-scatter.33.cloned.1.call-start = ((), (), s32[]{:S(2)}) async-start(), calls=%async_computation.32 | async-start | bytes 1081344
  1911.9 515.8 %reduce-scatter.25.cloned.1.call-start = ((), (), s32[]{:S(2)}) async-start(), calls=%async_computation.28 | async-start | bytes 20971520 | tf_op jit(solution)/shard_map/reduce_scatter | solution.py:293
  1927.8 783.2 %reduce-scatter.27.cloned.1.call-start = ((), (), s32[]{:S(2)}) async-start(), calls=%async_computation.29 | async-start | bytes 20971520 | tf_op jit(solution)/shard_map/reduce_scatter | solution.py:296
  1944.1 1050.2 %reduce-scatter.29.cloned.1.call-start = ((), (), s32[]{:S(2)}) async-start(), calls=%async_computation.30 | async-start | bytes 20971520 | tf_op jit(solution)/shard_map/reduce_scatter | solution.py:299
  1960.7 1397.6 %reduce-scatter.23.cloned.1.call-start = ((), (), s32[]{:S(2)}) async-start(), calls=%async_computation.27 | async-start | bytes 17301504 | tf_op jit(solution)/shard_map/reduce_scatter | solution.py:420
  1970.0 1753.0 %reduce-scatter.21.cloned.1.call-start = ((), (), s32[]{:S(2)}) async-start(), calls=%async_computation.26 | async-start | bytes 17301504 | tf_op jit(solution)/shard_map/reduce_scatter | solution.py:417
  1980.6 2107.1 %reduce-scatter.19.cloned.1.call-start = ((), (), s32[]{:S(2)}) async-start(), calls=%async_computation.25 | async-start | bytes 17301504 | tf_op jit(solution)/shard_map/reduce_scatter | solution.py:416
  1986.2 23.6 copy-start.34
  1986.2 23.6 copy-start.36
  2026.9 2425.6 %reduce-scatter.17.cloned.1.call-start = ((), (), s32[]{:S(2)}) async-start(), calls=%async_computation.24 | async-start | bytes 17301504 | tf_op jit(solution)/shard_map/reduce_scatter | solution.py:415
  2045.5 103.2 %copy-start.26 = (bf16[192,2048]{1,0:T(8,128)(2,1)S(1)}, bf16[192,2048]{1,0:T(8,128)(2,1)}, u32[]{:S(2)}) copy-start(bf16[192,2048]{1,0:T(8,128)(2,1)} %copy-done.25) | copy-start | bytes 2359300
  2161.7 46.6 %copy-start.16 = (f32[192,2048]{1,0:T(8,128)S(1)}, f32[192,2048]{1,0:T(8,128)}, u32[]{:S(2)}) copy-start(f32[192,2048]{1,0:T(8,128)} %copy-done.15) | copy-start | bytes 4718596
  2161.7 46.6 %copy-start.70 = (f32[192]{0:T(256)S(1)}, f32[192]{0:T(256)}, u32[]{:S(2)}) copy-start(f32[192]{0:T(256)} %get-tuple-element.61) | copy-start | bytes 2308
  (60 other events, 261.4 us)
Sparse Core Ops, SparseCore 0:
  9.6 152.5 all-gather.17
  163.8 147.7 all-gather.15
  313.2 147.7 all-gather.11
  463.0 63.5 all-gather.19
  528.6 61.9 all-gather.13
  592.0 148.2 all-gather.21
  741.8 284.9 all-gather.23
  1028.3 284.9 all-gather.25
  1314.9 284.9 all-gather.27
  1888.1 56.7 reduce-scatter.30
  1947.8 60.3 reduce-scatter.14
  2010.3 136.8 reduce-scatter.32
  2149.6 278.0 reduce-scatter.24
  2429.9 281.0 reduce-scatter.26
  2713.2 281.0 reduce-scatter.28
  2997.0 361.2 reduce-scatter.22
  3361.0 361.9 reduce-scatter.20
  3725.7 361.9 reduce-scatter.18
  4090.5 361.9 reduce-scatter.16
where the time goes:
time: 4470 us; the launch traced here: 4460 us
  waiting for transfers between devices  3730 us (83%)
  matrix products  269 us (6%)
  blocking collectives  189 us (4%)
  local copies, waits for them, and re-layouts  127 us (3%)
  other arithmetic  106 us (2%)
    reduce_scatter x1, waiting for transfers between devices, on_device(): lax.psum_scatter(query_w_grad, ('ep', 'fs'), scatter_dimension=0, tiled=T...  365 us
    reduce_scatter x1, waiting for transfers between devices, on_device(): lax.psum_scatter(key_w_grad, ('ep', 'fs'), scatter_dimension=0, tiled=True)  365 us
    reduce_scatter x1, waiting for transfers between devices, on_device(): lax.psum_scatter(value_w_grad, ('ep', 'fs'), scatter_dimension=0, tiled=T...  365 us
    reduce_scatter x1, waiting for transfers between devices, on_device(): lax.psum_scatter(output_w_grad, ('ep', 'fs'), scatter_dimension=0, tiled=...  357 us
    reduce_scatter x1, waiting for transfers between devices, on_device(): lax.psum_scatter(up_grad.astype(jnp.bfloat16), 'fs', scatter_dimension=1,...  277 us
    reduce_scatter x1, waiting for transfers between devices, on_device(): lax.psum_scatter(down_grad.astype(jnp.bfloat16), 'fs', scatter_dimension=...  277 us
    all_gather x1, waiting for transfers between devices, on_device(): lax.all_gather(w_up, 'fs', axis=1, tiled=True)  270 us
    all_gather x1, waiting for transfers between devices, on_device(): lax.all_gather(w_down, 'fs', axis=1, tiled=True)  270 us
  transfers between devices with their start and end apart: 22, of which 19 were waited for; matrix products, arithmetic and copies ran while one was open for 9% of the time, Pallas kernels for 0%

commit v1 on v0

v1 whole, which is shorter than its diff:
```python
import math

import jax
import jax.numpy as jnp
from jax import lax
from jax.experimental import pallas as pl
from jax.experimental.pallas import tpu as pltpu
from jax.sharding import PartitionSpec as P

epsilon = 1e-06
rope_base = 10000.0
masked_score = -1000000000.0
low_type = jnp.bfloat16
VMEM_LIMIT = 66_000_000


def rms_scale(values):
    return lax.rsqrt(jnp.mean(values * values, axis=-1, keepdims=True) + epsilon)


def mm(a, b, dims):
    return lax.dot_general(a, b, (dims, ((), ())), preferred_element_type=jnp.float32)


NN = ((1,), (0,))
NT = ((1,), (1,))
TN = ((0,), (0,))


def norm_back(values, scale, gain, upstream):
    weighted = upstream * gain
    inner_mean = jnp.mean(weighted * values, axis=-1, keepdims=True)
    return (
        scale * weighted - values * (scale * scale * scale) * inner_mean,
        upstream * values * scale,
    )


def group_layout(lengths_row, places_row, group_rows, span_rows):
    arrival = jnp.arange(group_rows, dtype=jnp.int32)
    span_hit = (arrival // span_rows)[:, None] == jnp.arange(places_row.shape[0], dtype=jnp.int32)[
        None, :
    ]
    places = (
        jnp.sum(jnp.where(span_hit, places_row[None, :], 0), axis=1) * span_rows
        + arrival % span_rows
    )
    seq_ends = jnp.cumsum(lengths_row)
    segment = jnp.sum((places[:, None] >= seq_ends[None, :]).astype(jnp.int32), axis=1)
    seq_starts = seq_ends - lengths_row
    picked = segment[:, None] == jnp.arange(lengths_row.shape[0], dtype=jnp.int32)[None, :]
    position = places - jnp.sum(jnp.where(picked, seq_starts[None, :], 0), axis=1)
    return (segment, position)


def rotated(pre, gain, cos2, sin2):
    scale = rms_scale(pre)
    normed = pre * scale * gain
    half = pre.shape[1] // 2
    return scale, normed * cos2 + pltpu.roll(normed, half, 1) * sin2


def attn_forward_kernel(
    q_ref, k_ref, v_ref, gq_ref, gk_ref, cos_ref, sin_ref, segc_ref, segr_ref, o_ref, q_scr, *, block
):
    rows = q_ref.shape[0]
    factor = 1.0 / math.sqrt(q_ref.shape[1])
    cos2 = cos_ref[...]
    sin2 = sin_ref[...]
    q_scr[...] = rotated(q_ref[...], gq_ref[...], cos2, sin2)[1].astype(low_type)
    key = rotated(k_ref[...], gk_ref[...], cos2, sin2)[1].astype(low_type)
    value = v_ref[...].astype(low_type)

    def step(i, carry):
        at = pl.ds(pl.multiple_of(i * block, block), block)
        raw = mm(q_scr[at, :], key, NT) * factor
        raw = jnp.where(segc_ref[at, :] == segr_ref[...], raw, masked_score)
        peak = jnp.max(raw, axis=1, keepdims=True)
        powers = jnp.exp(raw - peak)
        weights = powers / jnp.sum(powers, axis=1, keepdims=True)
        o_ref[at, :] = mm(weights.astype(low_type), value, NN).astype(low_type)
        return carry

    lax.fori_loop(0, rows // block, step, 0)


def attn_backward_kernel(
    q_ref,
    k_ref,
    v_ref,
    da_ref,
    gq_ref,
    gk_ref,
    cos_ref,
    sin_ref,
    segc_ref,
    segr_ref,
    dq_ref,
    dk_ref,
    dv_ref,
    dgq_ref,
    dgk_ref,
    q_scr,
    dq_scr,
    dk_scr,
    dv_scr,
    *,
    block,
):
    rows, head_dim = q_ref.shape
    factor = 1.0 / math.sqrt(head_dim)
    cos2 = cos_ref[...]
    sin2 = sin_ref[...]
    q_scale, q_rot = rotated(q_ref[...], gq_ref[...], cos2, sin2)
    q_scr[...] = q_rot.astype(low_type)
    k_scale, k_rot = rotated(k_ref[...], gk_ref[...], cos2, sin2)
    key = k_rot.astype(low_type)
    value = v_ref[...].astype(low_type)
    dk_scr[...] = jnp.zeros_like(dk_scr)
    dv_scr[...] = jnp.zeros_like(dv_scr)

    def step(i, carry):
        at = pl.ds(pl.multiple_of(i * block, block), block)
        query = q_scr[at, :]
        grads = da_ref[at, :]
        raw = mm(query, key, NT) * factor
        raw = jnp.where(segc_ref[at, :] == segr_ref[...], raw, masked_score)
        peak = jnp.max(raw, axis=1, keepdims=True)
        powers = jnp.exp(raw - peak)
        probs = powers / jnp.sum(powers, axis=1, keepdims=True)
        grad_probs = mm(grads, value, NT)
        delta = jnp.sum(probs * grad_probs, axis=1, keepdims=True)
        grad_scores = (probs * (grad_probs - delta)).astype(low_type)
        dq_scr[at, :] = mm(grad_scores, key, NN) * factor
        dk_scr[...] += mm(grad_scores, query, TN)
        dv_scr[...] += mm(probs.astype(low_type), grads, TN)
        return carry

    lax.fori_loop(0, rows // block, step, 0)
    half = head_dim // 2

    def finish(pre, scale, gain, upstream, out_ref, gain_out_ref):
        upstream = upstream.astype(low_type).astype(jnp.float32)
        back = upstream * cos2 - pltpu.roll(upstream, half, 1) * sin2
        grad_pre, gain_terms = norm_back(pre, scale, gain, back)
        out_ref[...] = grad_pre.astype(low_type)
        gain_out_ref[0] = jnp.sum(gain_terms, axis=0, keepdims=True)

    finish(q_ref[...], q_scale, gq_ref[...], dq_scr[...], dq_ref, dgq_ref)
    finish(k_ref[...], k_scale, gk_ref[...], dk_scr[...] * factor, dk_ref, dgk_ref)
    dv_ref[...] = dv_scr[...].astype(low_type)


def attention_forward(qkv, gain_q, gain_k, cos2, sin2, segment, head_dim):
    rows, width3 = qkv.shape
    heads = width3 // (3 * head_dim)
    block = 256
    col = lambda part: pl.BlockSpec((rows, head_dim), lambda h: (0, part * heads + h))
    full = lambda shape: pl.BlockSpec(shape, lambda h: (0, 0))
    return pl.pallas_call(
        lambda *refs: attn_forward_kernel(*refs, block=block),
        grid=(heads,),
        in_specs=[
            col(0),
            col(1),
            col(2),
            full((1, head_dim)),
            full((1, head_dim)),
            full((rows, head_dim)),
            full((rows, head_dim)),
            full((rows, 1)),
            full((1, rows)),
        ],
        out_specs=pl.BlockSpec((rows, head_dim), lambda h: (0, h)),
        out_shape=jax.ShapeDtypeStruct((rows, heads * head_dim), low_type),
        scratch_shapes=[pltpu.VMEM((rows, head_dim), low_type)],
        compiler_params=pltpu.CompilerParams(vmem_limit_bytes=VMEM_LIMIT // 2),
        cost_estimate=pl.CostEstimate(
            flops=heads * rows * rows * head_dim * 4,
            bytes_accessed=rows * width3 * 4,
            transcendentals=heads * rows * rows,
        ),
        name="attn_forward",
    )(qkv, qkv, qkv, gain_q, gain_k, cos2, sin2, segment[:, None], segment[None, :])


def attention_backward(qkv, grad_attended, gain_q, gain_k, cos2, sin2, segment, head_dim):
    rows, width3 = qkv.shape
    heads = width3 // (3 * head_dim)
    block = 256
    col = lambda part: pl.BlockSpec((rows, head_dim), lambda h: (0, part * heads + h))
    full = lambda shape: pl.BlockSpec(shape, lambda h: (0, 0))
    wide = jax.ShapeDtypeStruct((rows, heads * head_dim), low_type)
    gain = jax.ShapeDtypeStruct((heads, 1, head_dim), jnp.float32)
    gain_spec = pl.BlockSpec((1, 1, head_dim), lambda h: (h, 0, 0))
    return pl.pallas_call(
        lambda *refs: attn_backward_kernel(*refs, block=block),
        grid=(heads,),
        in_specs=[
            col(0),
            col(1),
            col(2),
            col(0),
            full((1, head_dim)),
            full((1, head_dim)),
            full((rows, head_dim)),
            full((rows, head_dim)),
            full((rows, 1)),
            full((1, rows)),
        ],
        out_specs=[col(0), col(0), col(0), gain_spec, gain_spec],
        out_shape=[wide, wide, wide, gain, gain],
        scratch_shapes=[
            pltpu.VMEM((rows, head_dim), low_type),
            pltpu.VMEM((rows, head_dim), jnp.float32),
            pltpu.VMEM((rows, head_dim), jnp.float32),
            pltpu.VMEM((rows, head_dim), jnp.float32),
        ],
        compiler_params=pltpu.CompilerParams(vmem_limit_bytes=VMEM_LIMIT // 2),
        cost_estimate=pl.CostEstimate(
            flops=heads * rows * rows * head_dim * 10,
            bytes_accessed=rows * width3 * 6,
            transcendentals=heads * rows * rows,
        ),
        name="attn_backward",
    )(qkv, qkv, qkv, grad_attended, gain_q, gain_k, cos2, sin2, segment[:, None], segment[None, :])


def experts_kernel(place_ref, *refs, sources, cap, locals_, total, shards):
    x_ref, g_ref, rank_ref, router_ref = refs[:4]
    refs = refs[4:]
    gate_refs, up_refs, wd_ref = refs[:shards], refs[shards : 2 * shards], refs[2 * shards]
    refs = refs[2 * shards + 1 :]
    out_hbm, dx_hbm, dwd_hbm = refs[:3]
    dwg_hbm, dwu_hbm = refs[3 : 3 + shards], refs[3 + shards : 3 + 2 * shards]
    refs = refs[3 + 2 * shards :]
    x_slots, g_slots, gates_col, acc_g, acc_u, acc_d, out_stage, dx_stage = refs[:8]
    out_sem, dx_sem, acc_sem, grad_sem = refs[8:]
    b = pl.program_id(0)
    e = pl.program_id(1)
    blocks = pl.num_programs(0)
    rows = x_ref.shape[0] // sources
    width = x_ref.shape[1]
    chunk = width // shards
    slots = sources * cap
    me = place_ref[1]

    def one_hot(s):
        slot = lax.broadcasted_iota(jnp.int32, (cap, rows), 0)
        return [slot == rank_ref[s, j : j + 1, :] for j in range(locals_)]

    @pl.when(e == 0)
    def _():
        for s in range(sources):
            at = pl.ds(s * rows, rows)
            logits = mm(router_ref[...], x_ref[at, :], NT)
            live = rank_ref[s] >= 0
            kept = jnp.where(live, logits, -1e30)
            powers = jnp.where(live, jnp.exp(kept - jnp.max(kept, axis=0, keepdims=True)), 0.0)
            gates = powers / jnp.sum(powers, axis=0, keepdims=True)
            hits = one_hot(s)
            for j in range(locals_):
                picked = jnp.sum(
                    jnp.where(hits[j], gates[j : j + 1, :], 0.0), axis=1, keepdims=True
                )
                gates_col[j, s * cap : (s + 1) * cap, :] = jnp.broadcast_to(
                    picked, (cap, gates_col.shape[2])
                )
            select = jnp.concatenate([h.astype(jnp.float32) for h in hits], axis=0).astype(low_type)
            for c in range(0, width, chunk):
                picked_x = mm(select, x_ref[at, c : c + chunk], NN).astype(low_type)
                picked_g = mm(select, g_ref[at, c : c + chunk], NN).astype(low_type)
                for j in range(locals_):
                    x_slots[j, s * cap : (s + 1) * cap, c : c + chunk] = picked_x[
                        j * cap : (j + 1) * cap
                    ]
                    g_slots[j, s * cap : (s + 1) * cap, c : c + chunk] = picked_g[
                        j * cap : (j + 1) * cap
                    ]

    @pl.when(b == 0)
    def _():
        acc_g[e] = jnp.zeros(acc_g.shape[1:], jnp.float32)
        acc_u[e] = jnp.zeros(acc_u.shape[1:], jnp.float32)
        acc_d[e] = jnp.zeros(acc_d.shape[1:], jnp.float32)

    hidden = wd_ref.shape[1]
    gate = gates_col[e][:, :1]
    gs = g_slots[e, :slots, :width]
    gate_pre = jnp.zeros((slots, hidden), jnp.float32)
    up_pre = jnp.zeros((slots, hidden), jnp.float32)
    columns = [
        pl.ds(pl.multiple_of(lax.rem(me + shards - k, shards) * chunk, chunk), chunk)
        for k in range(shards)
    ]
    for k in range(shards):
        xs = x_slots[e, :slots, columns[k]]
        gate_pre += mm(xs, gate_refs[k][0], NN)
        up_pre += mm(xs, up_refs[k][0], NN)
    back = mm(gs, wd_ref[0], NT)
    sigmoid = jax.nn.sigmoid(gate_pre)
    silu = gate_pre * sigmoid
    activated = silu * up_pre
    grad_gate_dot = jnp.sum(
        activated.astype(low_type).astype(jnp.float32) * back, axis=1, keepdims=True
    )
    grad_act = back * gate
    grad_up = (grad_act * silu).astype(low_type)
    grad_gate = (grad_act * up_pre * sigmoid * (1.0 + gate_pre * (1.0 - sigmoid))).astype(low_type)
    act_gated = (activated * gate).astype(low_type)
    for c in range(0, width, chunk):
        cols = pl.ds(c, chunk)
        acc_g[e, :, cols] += mm(grad_gate, x_slots[e, :slots, cols], TN)
        acc_u[e, :, cols] += mm(grad_up, x_slots[e, :slots, cols], TN)
        acc_d[e, :, cols] += mm(act_gated, g_slots[e, :slots, cols], TN)
    for c in range(0, width, chunk):
        cols = pl.ds(c, chunk)
        x_slots[e, :slots, cols] = mm(act_gated, wd_ref[0, :, cols], NN).astype(low_type)
    for k in range(shards):
        g_slots[e, :slots, columns[k]] = (
            mm(grad_gate, gate_refs[k][0], NT) + mm(grad_up, up_refs[k][0], NT)
        ).astype(low_type)
    lanes = g_slots.shape[2] - width
    lane = lax.broadcasted_iota(jnp.int32, (slots, lanes), 1)
    high = grad_gate_dot.astype(low_type).astype(jnp.float32)
    mine = place_ref[0] + e
    g_slots[e, :slots, width:] = jnp.where(
        lane == mine, high, jnp.where(lane == mine + total, grad_gate_dot - high, 0.0)
    ).astype(low_type)

    @pl.when(e == pl.num_programs(1) - 1)
    def _():
        pending = [None, None]
        for s in range(sources):
            slot = s % 2
            if pending[slot] is not None:
                for copy in pending[slot]:
                    copy.wait()
            hits = one_hot(s)
            select = jnp.concatenate([h.astype(jnp.float32) for h in hits], axis=0).astype(low_type)
            part = slice(s * cap, (s + 1) * cap)
            for c in range(0, width, chunk):
                cols = slice(c, c + chunk)
                ys = jnp.concatenate([x_slots[j, part, cols] for j in range(locals_)], axis=0)
                out_stage[slot, :, cols] = mm(select, ys, TN).astype(low_type)
                ds_ = jnp.concatenate([g_slots[j, part, cols] for j in range(locals_)], axis=0)
                dx_stage[slot, :, cols] = mm(select, ds_, TN).astype(low_type)
            tail = jnp.concatenate([g_slots[j, part, width:] for j in range(locals_)], axis=0)
            dx_stage[slot, :, width:] = mm(select, tail, TN).astype(low_type)
            at = pl.ds((b * sources + s) * rows, rows)
            copies = (
                pltpu.make_async_copy(out_stage.at[slot], out_hbm.at[at], out_sem.at[slot]),
                pltpu.make_async_copy(dx_stage.at[slot], dx_hbm.at[at], dx_sem.at[slot]),
            )
            for copy in copies:
                copy.start()
            pending[slot] = copies
        for copies in pending:
            if copies is not None:
                for copy in copies:
                    copy.wait()

    @pl.when((b == blocks - 1) & (e == locals_ - 1))
    def _():
        copies = [pltpu.make_async_copy(acc_d, dwd_hbm, acc_sem)]
        copies[0].start()
        for j in range(locals_):
            x_slots[j, :hidden, :] = acc_g[j].astype(low_type)
            g_slots[j, :hidden, :width] = acc_u[j].astype(low_type)
            for k in range(shards):
                cols = pl.ds(pl.multiple_of(lax.rem(me + k, shards) * chunk, chunk), chunk)
                for which, (held, target) in enumerate(((x_slots, dwg_hbm), (g_slots, dwu_hbm))):
                    copy = pltpu.make_async_copy(
                        held.at[j, pl.ds(0, hidden), cols],
                        target[k].at[j],
                        grad_sem.at[which, j, k],
                    )
                    copy.start()
                    copies.append(copy)
        for copy in copies:
            copy.wait()


def run_experts(place, x_all, g_all, rank, router_rows, gate_parts, up_parts, w_down, cap):
    tokens_all, width = x_all.shape
    devices, total, rows = rank.shape
    shards = len(gate_parts)
    locals_, shard_rows, hidden = gate_parts[0].shape
    sources = 4
    blocks = devices // sources
    block_rows = sources * rows
    slots = sources * cap
    held_rows = max(slots, hidden)
    any_spec = pl.BlockSpec(memory_space=pl.ANY)
    weight_spec = pl.BlockSpec((1, shard_rows, hidden), lambda b, e, *_: (e, 0, 0))
    grid_spec = pltpu.PrefetchScalarGridSpec(
        num_scalar_prefetch=1,
        grid=(blocks, locals_),
        in_specs=[
            pl.BlockSpec((block_rows, width), lambda b, e, *_: (b, 0)),
            pl.BlockSpec((block_rows, width), lambda b, e, *_: (b, 0)),
            pl.BlockSpec((sources, total, rows), lambda b, e, *_: (b, 0, 0)),
            pl.BlockSpec((total, width), lambda b, e, *_: (0, 0)),
            *([weight_spec] * (2 * shards)),
            pl.BlockSpec((1, hidden, width), lambda b, e, *_: (e, 0, 0)),
        ],
        out_specs=[any_spec] * (3 + 2 * shards),
        scratch_shapes=[
            pltpu.VMEM((locals_, held_rows, width), low_type),
            pltpu.VMEM((locals_, held_rows, width + 128), low_type),
            pltpu.VMEM((locals_, slots, 128), jnp.float32),
            pltpu.VMEM((locals_, hidden, width), jnp.float32),
            pltpu.VMEM((locals_, hidden, width), jnp.float32),
            pltpu.VMEM((locals_, hidden, width), jnp.float32),
            pltpu.VMEM((2, rows, width), low_type),
            pltpu.VMEM((2, rows, width + 128), low_type),
            pltpu.SemaphoreType.DMA((2,)),
            pltpu.SemaphoreType.DMA((2,)),
            pltpu.SemaphoreType.DMA,
            pltpu.SemaphoreType.DMA((2, locals_, shards)),
        ],
    )
    piece = jax.ShapeDtypeStruct((locals_, hidden, shard_rows), low_type)
    got = pl.pallas_call(
        lambda *refs: experts_kernel(
            *refs, sources=sources, cap=cap, locals_=locals_, total=total, shards=shards
        ),
        grid_spec=grid_spec,
        out_shape=[
            jax.ShapeDtypeStruct((tokens_all, width), low_type),
            jax.ShapeDtypeStruct((tokens_all, width + 128), low_type),
            jax.ShapeDtypeStruct((locals_, hidden, width), jnp.float32),
            *([piece] * (2 * shards)),
        ],
        input_output_aliases={1: 0},
        compiler_params=pltpu.CompilerParams(vmem_limit_bytes=VMEM_LIMIT),
        cost_estimate=pl.CostEstimate(
            flops=18 * blocks * locals_ * slots * width * hidden,
            bytes_accessed=tokens_all * width * 8,
            transcendentals=blocks * locals_ * slots * hidden,
        ),
        name="experts",
    )(place, x_all, g_all, rank, router_rows, *gate_parts, *up_parts, w_down)
    return got[0], got[1], got[2], got[3 : 3 + shards], got[3 + shards :]


def split_columns(me, weights, shards):
    locals_, rows, width = weights[0].shape
    part = width // shards

    def kernel(place_ref, *refs):
        count = len(refs) // 2
        for i in range(count):
            refs[count + i][...] = refs[i][...]

    def block(k):
        return pl.BlockSpec((1, rows, part), lambda e, at: (e, 0, lax.rem(at[0] + k, shards)))

    got = pl.pallas_call(
        kernel,
        grid_spec=pltpu.PrefetchScalarGridSpec(
            num_scalar_prefetch=1,
            grid=(locals_,),
            in_specs=[block(k) for _ in weights for k in range(shards)],
            out_specs=[pl.BlockSpec((1, rows, part), lambda e, at: (e, 0, 0))]
            * (len(weights) * shards),
        ),
        out_shape=[jax.ShapeDtypeStruct((locals_, rows, part), weights[0].dtype)]
        * (len(weights) * shards),
        cost_estimate=pl.CostEstimate(
            flops=0, bytes_accessed=4 * len(weights) * locals_ * rows * width, transcendentals=0
        ),
        name="split_columns",
    )(me, *[w for w in weights for _ in range(shards)])
    return [got[i * shards : (i + 1) * shards] for i in range(len(weights))]


def join_columns(me, parts):
    shards = len(parts)
    locals_, hidden, rows = parts[0].shape

    def kernel(place_ref, *refs):
        out_ref = refs[shards]
        for k in range(shards):

            @pl.when(pl.program_id(1) == k)
            def _():
                out_ref[0] = refs[k][0].astype(jnp.float32).T

    return pl.pallas_call(
        kernel,
        grid_spec=pltpu.PrefetchScalarGridSpec(
            num_scalar_prefetch=1,
            grid=(locals_, shards),
            in_specs=[pl.BlockSpec((1, hidden, rows), lambda e, k, at: (e, 0, 0))] * shards,
            out_specs=pl.BlockSpec(
                (1, rows, hidden), lambda e, k, at: (e, 0, lax.rem(at[0] + shards - k, shards))
            ),
        ),
        out_shape=jax.ShapeDtypeStruct((locals_, rows, shards * hidden), jnp.float32),
        cost_estimate=pl.CostEstimate(
            flops=0, bytes_accessed=6 * locals_ * rows * shards * hidden, transcendentals=0
        ),
        name="join_columns",
    )(me, *parts)


def shifted(values, count, step):
    return lax.ppermute(values, "fs", [(i, (i + step) % count) for i in range(count)])


def fs_exchange(pieces):
    count = pieces.shape[0]
    me = lax.axis_index("fs")
    result = jnp.zeros_like(pieces)
    result = lax.dynamic_update_index_in_dim(
        result, lax.dynamic_index_in_dim(pieces, me, 0, False), me, 0
    )
    for step in range(1, count):
        sent = lax.dynamic_index_in_dim(pieces, (me + step) % count, 0, False)
        result = lax.dynamic_update_index_in_dim(
            result, shifted(sent, count, step), (me - step) % count, 0
        )
    return result


def fs_gather(values):
    count = lax.axis_size("fs")
    me = lax.axis_index("fs")
    result = jnp.zeros((count,) + values.shape, values.dtype)
    for step in range(count):
        got = shifted(values, count, step) if step else values
        result = lax.dynamic_update_index_in_dim(result, got, (me - step) % count, 0)
    return result


def fs_sum(partial):
    count = lax.axis_size("fs")
    me = lax.axis_index("fs")
    rows = partial.shape[0] // count
    own = lax.dynamic_slice_in_dim(partial, me * rows, rows).astype(jnp.float32)
    for step in range(1, count):
        sent = lax.dynamic_slice_in_dim(partial, ((me + step) % count) * rows, rows)
        own = own + shifted(sent.astype(low_type), count, step).astype(jnp.float32)
    return own


def fs_send(parts):
    count = len(parts)
    return [parts[0]] + [shifted(parts[k], count, k) for k in range(1, count)]


def ep_flip(values, bit):
    count = lax.axis_size("ep")
    return lax.ppermute(values, "ep", [(i, i ^ (1 << bit)) for i in range(count)])


def ep_gather(values):
    bits = lax.axis_size("ep").bit_length() - 1
    me = lax.axis_index("ep")
    held = values
    order = range(bits - 1, -1, -1)
    for bit in order:
        got = ep_flip(held, bit)
        low = ((me >> bit) & 1) == 0
        held = jnp.stack([jnp.where(low, held, got), jnp.where(low, got, held)])
    held = jnp.transpose(held, (*range(bits - 1, -1, -1), *range(bits, held.ndim)))
    return held.reshape((1 << bits,) + values.shape)


def ep_sum(partial, after=None):
    count = lax.axis_size("ep")
    bits = count.bit_length() - 1
    me = lax.axis_index("ep")
    rows, columns = partial.shape[0] // count, partial.shape[1]

    if after is not None:
        me = me + (after[0, 0].astype(jnp.float32) * 0.0).astype(jnp.int32)

    def halve(held, bit, axis):
        mine = (me >> bit) & 1
        got = ep_flip(lax.dynamic_index_in_dim(held, 1 - mine, axis, False), bit)
        kept = lax.dynamic_index_in_dim(held, mine, axis, False)
        return (kept.astype(jnp.float32) + got.astype(jnp.float32)).astype(low_type)

    first = halve(partial.reshape(count // 2, 2, rows, columns), 0, 1)
    half = columns // 2 // 128 * 128
    results = []
    for start, stop, order in (
        (0, half, range(1, bits)),
        (half, columns, range(bits - 1, 0, -1)),
    ):
        held = first[:, :, start:stop].reshape((2,) * (bits - 1) + (rows, stop - start))
        left = list(range(bits - 1, 0, -1))
        for bit in order:
            held = halve(held, bit, left.index(bit))
            left.remove(bit)
        results.append(held)
    return jnp.concatenate(results, axis=1)


def on_device(
    tokens,
    attn_gain,
    w_query,
    w_key,
    w_value,
    query_gain,
    key_gain,
    w_output,
    ffn_gain,
    w_router,
    w_gate,
    w_up,
    w_down,
    seq_lengths,
    span_places,
    routes,
    out_grad,
):
    rows_dev, width = tokens.shape
    n_fs = lax.axis_size("fs")
    n_ep = lax.axis_size("ep")
    devices = n_fs * n_ep
    fs_at = lax.axis_index("fs")
    ep_at = lax.axis_index("ep")
    group_rows = rows_dev * n_fs
    shard_rows = width // n_fs
    head_dim = query_gain.shape[0] * n_fs
    head_width = width // n_fs
    local_experts = w_gate.shape[0]
    experts_total = local_experts * n_ep
    top_count = routes.shape[1]
    hidden = w_gate.shape[2] // n_fs
    capacity = 4 * rows_dev * top_count // (3 * experts_total)

    tokens_group = lax.all_gather(tokens, "fs", axis=0, tiled=True)
    small = jnp.concatenate(
        [w_router.reshape(-1), attn_gain, ffn_gain, query_gain, key_gain], axis=0
    )
    small = fs_gather(small)
    cut = shard_rows * experts_total
    router_full = small[:, :cut].reshape(width, experts_total)
    gain_one = small[:, cut : cut + shard_rows].reshape(width).astype(jnp.float32)
    cut += shard_rows
    gain_two = small[:, cut : cut + shard_rows].reshape(width).astype(jnp.float32)
    cut += shard_rows
    part = head_dim // n_fs
    gain_query = small[:, cut : cut + part].reshape(1, head_dim).astype(jnp.float32)
    cut += part
    gain_key = small[:, cut : cut + part].reshape(1, head_dim).astype(jnp.float32)

    share = shard_rows // n_ep
    heads_in = jnp.stack(
        [
            lax.dynamic_slice_in_dim(w, ep_at * share, share).reshape(share, n_fs, head_width)
            for w in (w_query, w_key, w_value)
        ],
        axis=2,
    )
    heads_in = fs_exchange(jnp.transpose(heads_in, (1, 0, 2, 3)))
    heads_in = ep_gather(heads_in)
    w_heads = jnp.transpose(heads_in, (1, 0, 2, 3, 4)).reshape(width, 3 * head_width)

    fs_place = fs_at.reshape(1).astype(jnp.int32)
    gate_send, up_send = split_columns(fs_place, (w_gate, w_up), n_fs)
    gate_parts = fs_send(gate_send)
    up_parts = fs_send(up_send)

    expert_ids = jnp.arange(experts_total, dtype=jnp.int32)
    hit = jnp.any(routes[:, :, None] == expert_ids[None, None, :], axis=1)
    before = jnp.arange(rows_dev, dtype=jnp.int32)
    upper = (before[:, None] <= before[None, :]).astype(low_type)
    counts = mm(hit.astype(low_type), upper, TN)
    rank = jnp.where(hit.T, counts.astype(jnp.int32) - 1, -1)
    wide = jnp.concatenate([out_grad, rank.T.astype(low_type)], axis=1)
    wide = jnp.pad(wide, ((0, 0), (0, 128 - experts_total)))
    grad_all = lax.all_gather(wide, ("ep", "fs"), axis=0, tiled=True)
    base = ep_at * local_experts
    rank_all = jnp.transpose(
        grad_all[:, width : width + experts_total].reshape(devices, rows_dev, experts_total),
        (0, 2, 1),
    ).astype(jnp.int32)
    rank_rolled = jnp.roll(rank_all, -base, axis=1)
    router_rows = jnp.roll(router_full.T, -base, axis=0)

    segment, position = group_layout(
        seq_lengths[0], span_places[0], group_rows, group_rows // span_places.shape[1]
    )
    half_dim = head_dim // 2
    inverse = jnp.exp(
        jnp.arange(half_dim).astype(jnp.float32) * (-2.0 * math.log(rope_base) / head_dim)
    )
    angles = position.astype(jnp.float32)[:, None] * inverse[None, :]
    cosines = jnp.cos(angles)
    sines = jnp.sin(angles)
    cos2 = jnp.concatenate([cosines, cosines], axis=1)
    sin2 = jnp.concatenate([-sines, sines], axis=1)
    group_in = tokens_group.astype(jnp.float32)
    group_scale = rms_scale(group_in)
    normed_group = (group_in * group_scale * gain_one).astype(low_type)
    qkv = mm(normed_group, w_heads, NN)
    attended = attention_forward(qkv, gain_query, gain_key, cos2, sin2, segment, head_dim)
    branch = fs_sum(mm(attended, w_output, NN).astype(low_type))
    hidden_in = tokens.astype(jnp.float32)
    scale_one = rms_scale(hidden_in)
    hidden_mid = hidden_in + branch
    scale_two = rms_scale(hidden_mid)
    normed_two = (hidden_mid * scale_two * gain_two).astype(low_type)

    normed_all = lax.all_gather(normed_two, ("ep", "fs"), axis=0, tiled=True)
    out_part, dx_part, dwd, dwg, dwu = run_experts(
        jnp.stack([base, fs_at]).astype(jnp.int32),
        normed_all,
        grad_all,
        rank_rolled,
        router_rows,
        gate_parts,
        up_parts,
        w_down,
        capacity,
    )
    dx_group = ep_sum(dx_part)
    dx_own = fs_sum(dx_group)
    gate_grad = join_columns(fs_place, fs_send(dwg))
    up_grad = join_columns(fs_place, fs_send(dwu))

    logits = mm(normed_two, router_full, NN)
    kept = jnp.where(hit, logits, -1e30)
    powers = jnp.where(hit, jnp.exp(kept - jnp.max(kept, axis=1, keepdims=True)), 0.0)
    gates = powers / jnp.sum(powers, axis=1, keepdims=True)
    grad_gates = (
        dx_own[:, width : width + experts_total]
        + dx_own[:, width + experts_total : width + 2 * experts_total]
    )
    weighted = gates * grad_gates
    grad_logits = (weighted - gates * jnp.sum(weighted, axis=1, keepdims=True)).astype(low_type)
    router_grad = mm(normed_two, grad_logits, TN)
    grad_normed_two = dx_own[:, :width] + mm(grad_logits, router_full, NT)
    grad_mid_norm, gain_two_terms = norm_back(hidden_mid, scale_two, gain_two, grad_normed_two)
    gain_two_grad = jnp.sum(gain_two_terms, axis=0)
    grad_mid = out_grad.astype(jnp.float32) + grad_mid_norm

    branch_group = lax.all_gather(grad_mid.astype(low_type), "fs", axis=0, tiled=True)
    grad_attended = mm(branch_group, w_output, NT).astype(low_type)
    output_w_grad = mm(attended, branch_group, TN).astype(low_type)
    dq, dk, dv, dgq, dgk = attention_backward(
        qkv, grad_attended, gain_query, gain_key, cos2, sin2, segment, head_dim
    )
    grad_qkv = jnp.concatenate([dq, dk, dv], axis=1)
    heads_w_grad = mm(normed_group, grad_qkv, TN).astype(low_type)
    grad_normed_part = mm(grad_qkv, w_heads, NT)
    gain_one_grad = jnp.sum(grad_normed_part * group_in * group_scale, axis=0)
    grad_normed_one = fs_sum(grad_normed_part.astype(low_type))
    grad_in_norm, _ = norm_back(hidden_in, scale_one, gain_one, grad_normed_one)
    tokens_grad = (grad_mid + grad_in_norm).astype(low_type)

    out_w = lax.psum_scatter(output_w_grad, "ep", scatter_dimension=0, tiled=True)
    out_w = lax.ppermute(
        out_w,
        ("ep", "fs"),
        [(e * n_fs + z, z * n_ep + e) for e in range(n_ep) for z in range(n_fs)],
    ).astype(jnp.float32)
    heads_w = lax.psum_scatter(heads_w_grad, "ep", scatter_dimension=0, tiled=True)
    heads_w = fs_exchange(heads_w.reshape(n_fs, width // devices, 3 * head_width))
    heads_w = jnp.transpose(
        heads_w.reshape(n_fs, width // devices, 3, head_width), (2, 1, 0, 3)
    ).reshape(3, width // devices, width).astype(jnp.float32)

    def spread(values):
        each = head_dim // devices
        return jnp.pad(values.reshape(devices, each), ((0, 0), (0, width // devices - each))).reshape(
            width, 1
        )

    sums = jnp.concatenate(
        [
            router_grad,
            gain_two_grad[:, None],
            gain_one_grad[:, None],
            spread(jnp.sum(dgq, axis=(0, 1))),
            spread(jnp.sum(dgk, axis=(0, 1))),
        ],
        axis=1,
    )
    sums = jnp.pad(sums, ((0, 0), (0, 128 - sums.shape[1])))
    sums = lax.psum_scatter(sums, ("ep", "fs"), scatter_dimension=0, tiled=True)
    each = head_dim // devices

    out_group = ep_sum(out_part, dx_group)
    output = (hidden_mid + fs_sum(out_group)).astype(low_type)
    return (
        output,
        tokens_grad,
        sums[:, experts_total + 1],
        heads_w[0],
        heads_w[1],
        heads_w[2],
        sums[:each, experts_total + 2],
        sums[:each, experts_total + 3],
        out_w,
        sums[:, experts_total],
        sums[:, :experts_total],
        gate_grad,
        up_grad,
        dwd,
    )


def solution(mesh):
    return jax.shard_map(
        on_device,
        mesh=mesh,
        in_specs=(
            P(("ep", "fs"), None),
            P("fs"),
            P("fs", None),
            P("fs", None),
            P("fs", None),
            P("fs"),
            P("fs"),
            P("fs", None),
            P("fs"),
            P("fs", None),
            P("ep", "fs", None),
            P("ep", "fs", None),
            P("ep", "fs", None),
            P("ep", None),
            P("ep", None),
            P(("ep", "fs"), None),
            P(("ep", "fs"), None),
        ),
        out_specs=(
            P(("ep", "fs"), None),
            P(("ep", "fs"), None),
            P(("ep", "fs")),
            P(("ep", "fs"), None),
            P(("ep", "fs"), None),
            P(("ep", "fs"), None),
            P(("ep", "fs")),
            P(("ep", "fs")),
            P(("ep", "fs"), None),
            P(("ep", "fs")),
            P(("ep", "fs"), None),
            P("ep", "fs", None),
            P("ep", "fs", None),
            P("ep", "fs", None),
        ),
        check_vma=False,
    )
```

time: 4470 us -> 1860 us (0.42)
  waiting for transfers between devices: 3730 us -> 1090 us
  Pallas kernels: 0 us -> 243 us
  starting transfers between devices: 16.4 us -> 258 us
  matrix products: 269 us -> 49.4 us
  blocking collectives: 189 us -> 0 us
    reduce_scatter x8 -> x2, waiting for transfers between devices: 2240 us -> 101 us  [the longest x1 63.6 us: on_device(): lax.psum_scatter(heads_w_grad, 'ep', scatter_dimension=0, tiled=True)]
    all_gather x9 -> x4, waiting for transfers between devices: 1270 us -> 94.3 us  [the longest x1 76.6 us: on_device(): lax.all_gather(grad_mid.astype(low_type), 'fs', axis=0, tiled=True)]
    ppermute x0 -> x47, waiting for transfers between devices: none -> 881 us  [the longest x33 595 us: shifted(): lax.ppermute(values, 'fs', [(i, (i + step) % count) for i in range(count)])]
    ppermute x0 -> x47, starting transfers between devices: none -> 258 us  [the longest x33 240 us: shifted(): lax.ppermute(values, 'fs', [(i, (i + step) % count) for i in range(count)])]
    pallas_call x0 -> x6, Pallas kernels: none -> 243 us  [the longest x1 183 us: run_experts(): pl.pallas_call(lambda *refs: experts_kernel(*refs, sources=sources, cap=c...]
    dot_general x29 -> x10, matrix products: 268 us -> 49.4 us  [mm(): lax.dot_general(a, b, (dims, ((), ())), preferred_element_type=jnp.float32)]
    all_to_all x3 -> x0, waiting for transfers between devices: 119 us -> none  [the longest x1 68.8 us: on_device(): lax.all_to_all(grad_received, 'ep', split_axis=0, concat_axis=0, tiled=True)]
    all_to_all x1 -> x0, blocking collectives: 97.5 us -> none  [on_device(): lax.all_to_all(send_rows, 'ep', split_axis=0, concat_axis=0, tiled=True)]
  transfers between devices with their start and end apart: 22 -> 54, of which waited for: 19 -> 32; matrix products, arithmetic and copies ran while one was open for 9% -> 8% of each run, Pallas kernels for 0% -> 2%
where the time goes in v1:
time: 1860 us; the launch traced here: 1850 us
  waiting for transfers between devices  1090 us (59%)
  starting transfers between devices  258 us (14%)
  Pallas kernels  243 us (13%)
  local copies, waits for them, and re-layouts  115 us (6%)
  other arithmetic  77 us (4%)
  matrix products  49.4 us (3%)
    ppermute x33, waiting for transfers between devices, shifted(): lax.ppermute(values, 'fs', [(i, (i + step) % count) for i in range(count)])  595 us
    ppermute x13, waiting for transfers between devices, ep_flip(): return lax.ppermute(values, 'ep', [(i, i ^ 1 << bit) for i in range(count)])  286 us
    ppermute x33, starting transfers between devices, shifted(): lax.ppermute(values, 'fs', [(i, (i + step) % count) for i in range(count)])  240 us
    pallas_call x1, Pallas kernels, run_experts(): pl.pallas_call(lambda *refs: experts_kernel(*refs, sources=sources, cap=c...  183 us
    all_gather x1, waiting for transfers between devices, on_device(): lax.all_gather(grad_mid.astype(low_type), 'fs', axis=0, tiled=True)  76.6 us
    reduce_scatter x1, waiting for transfers between devices, on_device(): lax.psum_scatter(heads_w_grad, 'ep', scatter_dimension=0, tiled=True)  63.6 us
    dot_general x10, matrix products, mm(): lax.dot_general(a, b, (dims, ((), ())), preferred_element_type=jnp.float32)  49.4 us
    convert_element_type x10, other arithmetic, halve(): return (kept.astype(jnp.float32) + got.astype(jnp.float32)).astype(low_type)  43.7 us
  transfers between devices with their start and end apart: 54, of which 32 were waited for; matrix products, arithmetic and copies ran while one was open for 8% of the time, Pallas kernels for 2%

profile of v1, /device:TPU:0, one launch (start us, length us, event | category | flops | bytes accessed | tf_op | source)
XLA Modules:
  0.0 1854.2 jit_solution(1253412859057552611)
XLA Ops:
  30.1 15.6 collective-permute-done.4
  47.3 17.6 collective-permute-done.6
  66.8 33.7 %collective-permute-done.7 = bf16[2,4,64,3,512]{4,2,3,1,0:T(8,128)(2,1)} collective-permute-done((bf16[2,4,64,3,512]{4,2,3,1,0:T(8,128)(2,1)S(1)}, bf16[2,4,64,3,512]{4,2,3,1,0:T(8,128)(2,1)}, u32[]{:S(2)}, u32[]{:S(2)}) %collective-permute-start.7) | collective-permute-done | bytes 1572896 | tf_op jit(solution)/shard_map/ppermute | solution.py:555
  105.0 21.3 %collective-permute-start = (bf16[17472]{0:T(1024)(128)(2,1)S(1)}, bf16[17472]{0:T(1024)(128)(2,1)S(1)}, u32[]{:S(2)}, u32[]{:S(2)}) collective-permute-start(bf16[17472]{0:T(1024)(128)(2,1)S(1)} %concatenate.35), channel_id=1, source_target_pairs={{0,1},{1,2},{2,3},{3,0},{4,5},{5,6},{6,7},{7,4},{8,9},{9,10},{10,1... | collective-permute-start | bytes 104840 | tf_op jit(solution)/shard_map/ppermute | solution.py:509
  145.2 12.2 copy.94
  163.8 17.5 fusion.27.refs_0_.refs_1_.refs_2_
  181.4 12.1 attn_forward.1
  200.1 67.0 %collective-permute-done.10 = bf16[192,2048]{1,0:T(8,128)(2,1)S(1)} collective-permute-done((bf16[192,2048]{1,0:T(8,128)(2,1)}, bf16[192,2048]{1,0:T(8,128)(2,1)S(1)}, u32[]{:S(2)}, u32[]{:S(2)}) %collective-permute-start.10) | collective-permute-done | bytes 786464 | tf_op jit(solution)/shard_map/ppermute | solution.py:509
  270.7 31.4 %collective-permute-done.9 = bf16[192,2048]{1,0:T(8,128)(2,1)S(1)} collective-permute-done((bf16[192,2048]{1,0:T(8,128)(2,1)}, bf16[192,2048]{1,0:T(8,128)(2,1)S(1)}, u32[]{:S(2)}, u32[]{:S(2)}) %collective-permute-start.9) | collective-permute-done | bytes 786464 | tf_op jit(solution)/shard_map/ppermute | solution.py:509
  313.4 39.6 %collective-permute-start.12 = (bf16[4,512,256]{2,1,0:T(8,128)(2,1)}, bf16[4,512,256]{2,1,0:T(8,128)(2,1)}, u32[]{:S(2)}, u32[]{:S(2)}) collective-permute-start(bf16[4,512,256]{2,1,0:T(8,128)(2,1)} %get-tuple-element.39), channel_id=1, source_target_pairs={{0,1},{1,2},{2,3},{3,0},{4,5},{5,6},{6,7},{7,4},{8,9},{9,10},{10,1... | collective-permute-start | bytes 3145736 | tf_op jit(solution)/shard_map/ppermute | solution.py:509
  357.9 31.6 %collective-permute-done.12.refs_6_ = bf16[4,512,256]{2,1,0:T(8,128)(2,1)} collective-permute-done((bf16[4,512,256]{2,1,0:T(8,128)(2,1)}, bf16[4,512,256]{2,1,0:T(8,128)(2,1)}, u32[]{:S(2)}, u32[]{:S(2)}) %collective-permute-start.12) | collective-permute-done | bytes 1048608 | tf_op jit(solution)/shard_map/ppermute | solution.py:509
  400.2 39.8 %collective-permute-done.13.refs_7_ = bf16[4,512,256]{2,1,0:T(8,128)(2,1)} collective-permute-done((bf16[4,512,256]{2,1,0:T(8,128)(2,1)}, bf16[4,512,256]{2,1,0:T(8,128)(2,1)}, u32[]{:S(2)}, u32[]{:S(2)}) %collective-permute-start.13) | collective-permute-done | bytes 1048608 | tf_op jit(solution)/shard_map/ppermute | solution.py:509
  439.9 20.4 %collective-permute-done.14.refs_8_ = bf16[4,512,256]{2,1,0:T(8,128)(2,1)} collective-permute-done((bf16[4,512,256]{2,1,0:T(8,128)(2,1)}, bf16[4,512,256]{2,1,0:T(8,128)(2,1)}, u32[]{:S(2)}, u32[]{:S(2)}) %collective-permute-start.14) | collective-permute-done | bytes 1048608 | tf_op jit(solution)/shard_map/ppermute | solution.py:509
  460.4 33.7 %collective-permute-done.15.refs_10_ = bf16[4,512,256]{2,1,0:T(8,128)(2,1)} collective-permute-done((bf16[4,512,256]{2,1,0:T(8,128)(2,1)}, bf16[4,512,256]{2,1,0:T(8,128)(2,1)}, u32[]{:S(2)}, u32[]{:S(2)}) %collective-permute-start.15) | collective-permute-done | bytes 1048608 | tf_op jit(solution)/shard_map/ppermute | solution.py:509
  494.1 101.1 %collective-permute-done.16.refs_11_ = bf16[4,512,256]{2,1,0:T(8,128)(2,1)} collective-permute-done((bf16[4,512,256]{2,1,0:T(8,128)(2,1)}, bf16[4,512,256]{2,1,0:T(8,128)(2,1)}, u32[]{:S(2)}, u32[]{:S(2)}) %collective-permute-start.16) | collective-permute-done | bytes 1048608 | tf_op jit(solution)/shard_map/ppermute | solution.py:509
  595.2 17.7 all-gather.7.cloned.1.call-done.refs_1_
  612.9 182.7 %experts.1 = (bf16[6144,2048]{1,0:T(8,128)(2,1)}, bf16[6144,2176]{1,0:T(8,128)(2,1)}, f32[4,256,2048]{2,1,0:T(8,128)}, bf16[4,256,512]{2,1,0:T(8,128)(2,1)}, bf1...) custom-call(s32[2]{0:T(128)} %pad_add_fusion.refs_0_, ...), custom_call_target="tpu_custom_call", output_to_operand_aliasing={{0}: (1, {})} | custom-call | flops 77309411328 | bytes 100663296 | tf_op jit(solution)/shard_map/experts/pallas_call | solution.py:424
  795.6 11.0 dynamic-slice_bitcast_fusion
  806.8 20.4 %collective-permute-done.18 = bf16[4,768,2176]{2,1,0:T(8,128)(2,1)} collective-permute-done((bf16[4,768,2176]{2,1,0:T(8,128)(2,1)}, bf16[4,768,2176]{2,1,0:T(8,128)(2,1)}, u32[]{:S(2)}, u32[]{:S(2)}) %collective-permute-start.18) | collective-permute-done | bytes 13369376 | tf_op jit(solution)/shard_map/ppermute | solution.py:555
  827.2 10.6 fusion
  847.9 68.9 %collective-permute-done.19 = bf16[2,768,1024]{2,1,0:T(8,128)(2,1)} collective-permute-done((bf16[2,768,1024]{2,1,0:T(8,128)(2,1)S(1)}, bf16[2,768,1024]{2,1,0:T(8,128)(2,1)}, u32[]{:S(2)}, u32[]{:S(2)}) %collective-permute-start.19) | collective-permute-done | bytes 3145760 | tf_op jit(solution)/shard_map/ppermute | solution.py:555
  924.5 34.3 %collective-permute-done.20 = bf16[768,1024]{1,0:T(8,128)(2,1)} collective-permute-done((bf16[768,1024]{1,0:T(8,128)(2,1)S(1)}, bf16[768,1024]{1,0:T(8,128)(2,1)}, u32[]{:S(2)}, u32[]{:S(2)}) %collective-permute-start.20) | collective-permute-done | bytes 1572896 | tf_op jit(solution)/shard_map/ppermute | solution.py:555
  963.8 12.8 dynamic-slice_bitcast_fusion.1
  984.0 12.1 collective-permute-done.21
  996.1 10.8 fusion.1
  1021.0 41.0 %collective-permute-done.29 = bf16[2,768,1152]{2,1,0:T(8,128)(2,1)} collective-permute-done((bf16[2,768,1152]{2,1,0:T(8,128)(2,1)S(1)}, bf16[2,768,1152]{2,1,0:T(8,128)(2,1)}, u32[]{:S(2)}, u32[]{:S(2)}) %collective-permute-start.29) | collective-permute-done | bytes 3538976 | tf_op jit(solution)/shard_map/ppermute | solution.py:555
  1070.7 58.3 %collective-permute-done.24 = bf16[2,768,1024]{2,1,0:T(8,128)(2,1)} collective-permute-done((bf16[2,768,1024]{2,1,0:T(8,128)(2,1)}, bf16[2,768,1024]{2,1,0:T(8,128)(2,1)}, u32[]{:S(2)}, u32[]{:S(2)}) %collective-permute-start.24) | collective-permute-done | bytes 3145760 | tf_op jit(solution)/shard_map/ppermute | solution.py:555
  1143.3 38.5 %collective-permute-start.31 = (bf16[192,2176]{1,0:T(8,128)(2,1)S(1)}, bf16[192,2176]{1,0:T(8,128)(2,1)S(1)}, u32[]{:S(2)}, u32[]{:S(2)}) collective-permute-start(bf16[192,2176]{1,0:T(8,128)(2,1)S(1)} %get-tuple-element.76), channel_id=1, source_target_pairs={{0,1},{1,2},{2,3},{3,0},{4,5},{5,6},{6,7},{7,4},{8,9},{9,10},{10,1... | collective-permute-start | bytes 2506760 | tf_op jit(solution)/shard_map/ppermute | solution.py:509
  1186.9 27.0 %collective-permute-start.26 = (bf16[192,2048]{1,0:T(8,128)(2,1)S(1)}, bf16[192,2048]{1,0:T(8,128)(2,1)S(1)}, u32[]{:S(2)}, u32[]{:S(2)}) collective-permute-start(bf16[192,2048]{1,0:T(8,128)(2,1)S(1)} %get-tuple-element.82), channel_id=1, source_target_pairs={{0,1},{1,2},{2,3},{3,0},{4,5},{5,6},{6,7},{7,4},{8,9},{9,10},{10,1... | collective-permute-start | bytes 2359304 | tf_op jit(solution)/shard_map/ppermute | solution.py:509
  1217.4 22.7 %collective-permute-done.32 = bf16[192,2176]{1,0:T(8,128)(2,1)S(1)} collective-permute-done((bf16[192,2176]{1,0:T(8,128)(2,1)S(1)}, bf16[192,2176]{1,0:T(8,128)(2,1)S(1)}, u32[]{:S(2)}, u32[]{:S(2)}) %collective-permute-start.32) | collective-permute-done | bytes 835616 | tf_op jit(solution)/shard_map/ppermute | solution.py:509
  1241.6 15.4 collective-permute-done.26
  1257.0 50.0 %collective-permute-done.27 = bf16[192,2048]{1,0:T(8,128)(2,1)S(1)} collective-permute-done((bf16[192,2048]{1,0:T(8,128)(2,1)S(1)}, bf16[192,2048]{1,0:T(8,128)(2,1)S(1)}, u32[]{:S(2)}, u32[]{:S(2)}) %collective-permute-start.27) | collective-permute-done | bytes 786464 | tf_op jit(solution)/shard_map/ppermute | solution.py:509
  1310.1 76.6 %all-gather.11.cloned.1.call-done = bf16[768,2048]{1,0:T(8,128)(2,1)} async-done(((bf16[192,2048]{1,0:T(8,128)(2,1)}), bf16[768,2048]{1,0:T(8,128)(2,1)}) %all-gather.11.cloned.1.call-update) | async-done | bytes 3145744 | tf_op jit(solution)/shard_map/all_gather | solution.py:744
  1393.5 18.3 attn_backward.1
  1415.7 9.3 fusion.7
  1432.0 9.4 convolution_convert_fusion
  1447.3 24.1 %collective-permute-done.44.refs_1_ = bf16[4,256,512]{2,1,0:T(8,128)(2,1)} collective-permute-done((bf16[4,256,512]{2,1,0:T(8,128)(2,1)}, bf16[4,256,512]{2,1,0:T(8,128)(2,1)}, u32[]{:S(2)}, u32[]{:S(2)}) %collective-permute-start.44) | collective-permute-done | bytes 1048608 | tf_op jit(solution)/shard_map/ppermute | solution.py:509
  1472.9 44.2 %collective-permute-done.45.refs_2_ = bf16[4,256,512]{2,1,0:T(8,128)(2,1)S(1)} collective-permute-done((bf16[4,256,512]{2,1,0:T(8,128)(2,1)}, bf16[4,256,512]{2,1,0:T(8,128)(2,1)S(1)}, u32[]{:S(2)}, u32[]{:S(2)}) %collective-permute-start.45) | collective-permute-done | bytes 1048608 | tf_op jit(solution)/shard_map/ppermute | solution.py:509
  1517.1 38.3 %collective-permute-start.34 = (bf16[192,2048]{1,0:T(8,128)(2,1)}, bf16[192,2048]{1,0:T(8,128)(2,1)S(1)}, u32[]{:S(2)}, u32[]{:S(2)}) collective-permute-start(bf16[192,2048]{1,0:T(8,128)(2,1)} %get-tuple-element.79), channel_id=1, source_target_pairs={{0,1},{1,2},{2,3},{3,0},{4,5},{5,6},{6,7},{7,4},{8,9},{9,10},{10,1... | collective-permute-start | bytes 2359304 | tf_op jit(solution)/shard_map/ppermute | solution.py:509
  1555.4 32.8 %collective-permute-start.35 = (bf16[192,2048]{1,0:T(8,128)(2,1)}, bf16[192,2048]{1,0:T(8,128)(2,1)S(1)}, u32[]{:S(2)}, u32[]{:S(2)}) collective-permute-start(bf16[192,2048]{1,0:T(8,128)(2,1)} %get-tuple-element.81), channel_id=1, source_target_pairs={{0,2},{1,3},{2,0},{3,1},{4,6},{5,7},{6,4},{7,5},{8,10},{9,11},{10,... | collective-permute-start | bytes 2359304 | tf_op jit(solution)/shard_map/ppermute | solution.py:509
  1591.6 11.3 join_columns.3
  1602.9 43.5 %collective-permute-done.42.refs_2_ = bf16[4,256,512]{2,1,0:T(8,128)(2,1)} collective-permute-done((bf16[4,256,512]{2,1,0:T(8,128)(2,1)}, bf16[4,256,512]{2,1,0:T(8,128)(2,1)}, u32[]{:S(2)}, u32[]{:S(2)}) %collective-permute-start.42) | collective-permute-done | bytes 1048608 | tf_op jit(solution)/shard_map/ppermute | solution.py:509
  1646.4 11.4 join_columns.2
  1657.8 36.1 %collective-permute-done.35 = bf16[192,2048]{1,0:T(8,128)(2,1)S(1)} collective-permute-done((bf16[192,2048]{1,0:T(8,128)(2,1)}, bf16[192,2048]{1,0:T(8,128)(2,1)S(1)}, u32[]{:S(2)}, u32[]{:S(2)}) %collective-permute-start.35) | collective-permute-done | bytes 786464 | tf_op jit(solution)/shard_map/ppermute | solution.py:509
  1698.6 17.9 reduce-scatter.10.cloned.1.call-done
  1720.0 37.1 %reduce-scatter.8.cloned.1.call-done = bf16[64,2048]{1,0:T(8,128)(2,1)} async-done(((bf16[512,2048]{1,0:T(8,128)(2,1)}), bf16[64,2048]{1,0:T(8,128)(2,1)}) %reduce-scatter.8.cloned.1.call-update) | async-done | bytes 262160 | tf_op jit(solution)/shard_map/reduce_scatter | solution.py:758
  1758.7 63.6 %reduce-scatter.6.cloned.1.call-done = bf16[256,1536]{1,0:T(8,128)(2,1)} async-done(((bf16[2048,1536]{1,0:T(8,128)(2,1)}), bf16[256,1536]{1,0:T(8,128)(2,1)}) %reduce-scatter.6.cloned.1.call-update) | async-done | bytes 786448 | tf_op jit(solution)/shard_map/reduce_scatter | solution.py:764
  1832.2 8.3 collective-permute-done.38
  (366 shorter events, 226.8 us)
Async XLA Ops:
  7.2 129.4 %all-gather.5.cloned.1.call-start = ((), (), s32[]{:S(2)}) async-start(), calls=%async_computation.3 | async-start | bytes 3932160 | tf_op jit(solution)/shard_map/all_gather | solution.py:637
  7.9 388.6 %all-gather.9.cloned.1.call-start = ((), (), s32[]{:S(2)}) async-start(), calls=%async_computation.5 | async-start | bytes 27574272 | tf_op jit(solution)/shard_map/all_gather | solution.py:678
  11.8 601.1 %all-gather.7.cloned.1.call-start = ((), (), s32[]{:S(2)}) async-start(), calls=%async_computation.4 | async-start | bytes 25952256 | tf_op jit(solution)/shard_map/all_gather | solution.py:711
  19.7 26.0 %collective-permute-start.4 = (bf16[64,3,512]{2,0,1:T(8,128)(2,1)S(1)}, bf16[64,3,512]{2,0,1:T(8,128)(2,1)S(1)}, u32[]{:S(2)}, u32[]{:S(2)}) collective-permute-start(bf16[64,3,512]{2,0,1:T(8,128)(2,1)S(1)} %bitcast.205), channel_id=1, source_target_pairs={{0,2},{1,3},{2,0},{3,1},{4,6},{5,7},{6,4},{7,5},{8,10},{9,11},{10,... | collective-permute-start | bytes 589832 | tf_op jit(solution)/shard_map/ppermute | solution.py:509
  22.3 23.3 %collective-permute-start.5 = (bf16[64,3,512]{2,0,1:T(8,128)(2,1)S(1)}, bf16[64,3,512]{2,0,1:T(8,128)(2,1)S(1)}, u32[]{:S(2)}, u32[]{:S(2)}) collective-permute-start(bf16[64,3,512]{2,0,1:T(8,128)(2,1)S(1)} %bitcast.204), channel_id=1, source_target_pairs={{0,3},{1,0},{2,1},{3,2},{4,7},{5,4},{6,5},{7,6},{8,11},{9,8},{10,9... | collective-permute-start | bytes 589832 | tf_op jit(solution)/shard_map/ppermute | solution.py:509
  45.7 19.1 %collective-permute-start.6 = (bf16[4,64,3,512]{3,1,2,0:T(8,128)(2,1)S(1)}, bf16[4,64,3,512]{3,1,2,0:T(8,128)(2,1)S(1)}, u32[]{:S(2)}, u32[]{:S(2)}) collective-permute-start(bf16[4,64,3,512]{3,1,2,0:T(8,128)(2,1)S(1)} %bitcast_dynamic-update-slice_fusion.4), channel_id=1, source_target_pairs={{0,16},{4,20},{8,24},{12,28},{16,0},{20,4},{24,8},{28,12},{1,17},{... | collective-permute-start | bytes 2359304 | tf_op jit(solution)/shard_map/ppermute | solution.py:555
  65.1 35.5 %collective-permute-start.7 = (bf16[2,4,64,3,512]{4,2,3,1,0:T(8,128)(2,1)S(1)}, bf16[2,4,64,3,512]{4,2,3,1,0:T(8,128)(2,1)}, u32[]{:S(2)}, u32[]{:S(2)}) collective-permute-start(bf16[2,4,64,3,512]{4,2,3,1,0:T(8,128)(2,1)S(1)} %pad_maximum_fusion.2), channel_id=1, source_target_pairs={{0,8},{4,12},{8,0},{12,4},{16,24},{20,28},{24,16},{28,20},{1,9},{5... | collective-permute-start | bytes 4718600 | tf_op jit(solution)/shard_map/ppermute | solution.py:555
  104.6 34.7 %collective-permute-start.8 = (bf16[2,2,4,64,3,512]{5,3,4,2,0,1:T(8,128)(2,1)}, bf16[2,2,4,64,3,512]{5,3,4,2,0,1:T(8,128)(2,1)}, u32[]{:S(2)}, u32[]{:S(2)}) collective-permute-start(bf16[2,2,4,64,3,512]{5,3,4,2,0,1:T(8,128)(2,1)} %pad_maximum_fusion.1), channel_id=1, source_target_pairs={{0,4},{4,0},{8,12},{12,8},{16,20},{20,16},{24,28},{28,24},{1,5},{5... | collective-permute-start | bytes 9437192 | tf_op jit(solution)/shard_map/ppermute | solution.py:555
  105.0 27.5 %collective-permute-start = (bf16[17472]{0:T(1024)(128)(2,1)S(1)}, bf16[17472]{0:T(1024)(128)(2,1)S(1)}, u32[]{:S(2)}, u32[]{:S(2)}) collective-permute-start(bf16[17472]{0:T(1024)(128)(2,1)S(1)} %concatenate.35), channel_id=1, source_target_pairs={{0,1},{1,2},{2,3},{3,0},{4,5},{5,6},{6,7},{7,4},{8,9},{9,10},{10,1... | collective-permute-start | bytes 104840 | tf_op jit(solution)/shard_map/ppermute | solution.py:509
  197.7 69.4 %collective-permute-start.10 = (bf16[192,2048]{1,0:T(8,128)(2,1)}, bf16[192,2048]{1,0:T(8,128)(2,1)S(1)}, u32[]{:S(2)}, u32[]{:S(2)}) collective-permute-start(bf16[192,2048]{1,0:T(8,128)(2,1)} %get-tuple-element.87), channel_id=1, source_target_pairs={{0,2},{1,3},{2,0},{3,1},{4,6},{5,7},{6,4},{7,5},{8,10},{9,11},{10,... | collective-permute-start | bytes 2359304 | tf_op jit(solution)/shard_map/ppermute | solution.py:509
  198.0 72.7 %collective-permute-start.11 = (bf16[192,2048]{1,0:T(8,128)(2,1)}, bf16[192,2048]{1,0:T(8,128)(2,1)S(1)}, u32[]{:S(2)}, u32[]{:S(2)}) collective-permute-start(bf16[192,2048]{1,0:T(8,128)(2,1)} %get-tuple-element.86), channel_id=1, source_target_pairs={{0,3},{1,0},{2,1},{3,2},{4,7},{5,4},{6,5},{7,6},{8,11},{9,8},{10,9... | collective-permute-start | bytes 2359304 | tf_op jit(solution)/shard_map/ppermute | solution.py:509
  199.6 102.6 %collective-permute-start.9 = (bf16[192,2048]{1,0:T(8,128)(2,1)}, bf16[192,2048]{1,0:T(8,128)(2,1)S(1)}, u32[]{:S(2)}, u32[]{:S(2)}) collective-permute-start(bf16[192,2048]{1,0:T(8,128)(2,1)} %get-tuple-element.85), channel_id=1, source_target_pairs={{0,1},{1,2},{2,3},{3,0},{4,5},{5,6},{6,7},{7,4},{8,9},{9,10},{10,1... | collective-permute-start | bytes 2359304 | tf_op jit(solution)/shard_map/ppermute | solution.py:509
  306.2 1080.5 %all-gather.11.cloned.1.call-start = ((), (), s32[]{:S(2)}) async-start(), calls=%async_computation.6 | async-start | bytes 3932160 | tf_op jit(solution)/shard_map/all_gather | solution.py:744
  313.4 76.1 %collective-permute-start.12 = (bf16[4,512,256]{2,1,0:T(8,128)(2,1)}, bf16[4,512,256]{2,1,0:T(8,128)(2,1)}, u32[]{:S(2)}, u32[]{:S(2)}) collective-permute-start(bf16[4,512,256]{2,1,0:T(8,128)(2,1)} %get-tuple-element.39), channel_id=1, source_target_pairs={{0,1},{1,2},{2,3},{3,0},{4,5},{5,6},{6,7},{7,4},{8,9},{9,10},{10,1... | collective-permute-start | bytes 3145736 | tf_op jit(solution)/shard_map/ppermute | solution.py:509
  352.9 87.0 %collective-permute-start.13 = (bf16[4,512,256]{2,1,0:T(8,128)(2,1)}, bf16[4,512,256]{2,1,0:T(8,128)(2,1)}, u32[]{:S(2)}, u32[]{:S(2)}) collective-permute-start(bf16[4,512,256]{2,1,0:T(8,128)(2,1)} %get-tuple-element.40), channel_id=1, source_target_pairs={{0,2},{1,3},{2,0},{3,1},{4,6},{5,7},{6,4},{7,5},{8,10},{9,11},{10,... | collective-permute-start | bytes 3145736 | tf_op jit(solution)/shard_map/ppermute | solution.py:509
  352.9 107.4 %collective-permute-start.14 = (bf16[4,512,256]{2,1,0:T(8,128)(2,1)}, bf16[4,512,256]{2,1,0:T(8,128)(2,1)}, u32[]{:S(2)}, u32[]{:S(2)}) collective-permute-start(bf16[4,512,256]{2,1,0:T(8,128)(2,1)} %get-tuple-element.41), channel_id=1, source_target_pairs={{0,3},{1,0},{2,1},{3,2},{4,7},{5,4},{6,5},{7,6},{8,11},{9,8},{10,9... | collective-permute-start | bytes 3145736 | tf_op jit(solution)/shard_map/ppermute | solution.py:509
  355.4 138.7 %collective-permute-start.15 = (bf16[4,512,256]{2,1,0:T(8,128)(2,1)}, bf16[4,512,256]{2,1,0:T(8,128)(2,1)}, u32[]{:S(2)}, u32[]{:S(2)}) collective-permute-start(bf16[4,512,256]{2,1,0:T(8,128)(2,1)} %get-tuple-element.43), channel_id=1, source_target_pairs={{0,1},{1,2},{2,3},{3,0},{4,5},{5,6},{6,7},{7,4},{8,9},{9,10},{10,1... | collective-permute-start | bytes 3145736 | tf_op jit(solution)/shard_map/ppermute | solution.py:509
  355.4 239.8 %collective-permute-start.16 = (bf16[4,512,256]{2,1,0:T(8,128)(2,1)}, bf16[4,512,256]{2,1,0:T(8,128)(2,1)}, u32[]{:S(2)}, u32[]{:S(2)}) collective-permute-start(bf16[4,512,256]{2,1,0:T(8,128)(2,1)} %get-tuple-element.44), channel_id=1, source_target_pairs={{0,2},{1,3},{2,0},{3,1},{4,6},{5,7},{6,4},{7,5},{8,10},{9,11},{10,... | collective-permute-start | bytes 3145736 | tf_op jit(solution)/shard_map/ppermute | solution.py:509
  389.5 205.7 %collective-permute-start.17 = (bf16[4,512,256]{2,1,0:T(8,128)(2,1)}, bf16[4,512,256]{2,1,0:T(8,128)(2,1)}, u32[]{:S(2)}, u32[]{:S(2)}) collective-permute-start(bf16[4,512,256]{2,1,0:T(8,128)(2,1)} %get-tuple-element.45), channel_id=1, source_target_pairs={{0,3},{1,0},{2,1},{3,2},{4,7},{5,4},{6,5},{7,6},{8,11},{9,8},{10,9... | collective-permute-start | bytes 3145736 | tf_op jit(solution)/shard_map/ppermute | solution.py:509
  806.6 20.6 %collective-permute-start.18 = (bf16[4,768,2176]{2,1,0:T(8,128)(2,1)}, bf16[4,768,2176]{2,1,0:T(8,128)(2,1)}, u32[]{:S(2)}, u32[]{:S(2)}) collective-permute-start(bf16[4,768,2176]{2,1,0:T(8,128)(2,1)} %dynamic-slice_bitcast_fusion), channel_id=1, source_target_pairs={{0,4},{4,0},{8,12},{12,8},{16,20},{20,16},{24,28},{28,24},{1,5},{5... | collective-permute-start | bytes 40108040 | tf_op jit(solution)/shard_map/ppermute | solution.py:555
  846.4 70.4 %collective-permute-start.19 = (bf16[2,768,1024]{2,1,0:T(8,128)(2,1)S(1)}, bf16[2,768,1024]{2,1,0:T(8,128)(2,1)}, u32[]{:S(2)}, u32[]{:S(2)}) collective-permute-start(bf16[2,768,1024]{2,1,0:T(8,128)(2,1)S(1)} %dynamic-slice_bitcast_fusion.5), channel_id=1, source_target_pairs={{0,8},{4,12},{8,0},{12,4},{16,24},{20,28},{24,16},{28,20},{1,9},{5... | collective-permute-start | bytes 9437192 | tf_op jit(solution)/shard_map/ppermute | solution.py:555
  923.0 35.9 %collective-permute-start.20 = (bf16[768,1024]{1,0:T(8,128)(2,1)S(1)}, bf16[768,1024]{1,0:T(8,128)(2,1)}, u32[]{:S(2)}, u32[]{:S(2)}) collective-permute-start(bf16[768,1024]{1,0:T(8,128)(2,1)S(1)} %dynamic-slice_bitcast_fusion.9), channel_id=1, source_target_pairs={{0,16},{4,20},{8,24},{12,28},{16,0},{20,4},{24,8},{28,12},{1,17},{... | collective-permute-start | bytes 4718600 | tf_op jit(solution)/shard_map/ppermute | solution.py:555
  976.6 19.5 %collective-permute-start.21 = (bf16[4,768,2048]{2,1,0:T(8,128)(2,1)}, bf16[4,768,2048]{2,1,0:T(8,128)(2,1)}, u32[]{:S(2)}, u32[]{:S(2)}) collective-permute-start(bf16[4,768,2048]{2,1,0:T(8,128)(2,1)} %dynamic-slice_bitcast_fusion.1), channel_id=1, source_target_pairs={{0,4},{4,0},{8,12},{12,8},{16,20},{20,16},{24,28},{28,24},{1,5},{5... | collective-permute-start | bytes 37748744 | tf_op jit(solution)/shard_map/ppermute | solution.py:555
  982.5 79.6 %collective-permute-start.29 = (bf16[2,768,1152]{2,1,0:T(8,128)(2,1)S(1)}, bf16[2,768,1152]{2,1,0:T(8,128)(2,1)}, u32[]{:S(2)}, u32[]{:S(2)}) collective-permute-start(bf16[2,768,1152]{2,1,0:T(8,128)(2,1)S(1)} %dynamic-slice_bitcast_fusion.2), channel_id=1, source_target_pairs={{0,16},{4,20},{8,24},{12,28},{16,0},{20,4},{24,8},{28,12},{1,17},{... | collective-permute-start | bytes 10616840 | tf_op jit(solution)/shard_map/ppermute | solution.py:555
  1014.1 114.8 %collective-permute-start.24 = (bf16[2,768,1024]{2,1,0:T(8,128)(2,1)}, bf16[2,768,1024]{2,1,0:T(8,128)(2,1)}, u32[]{:S(2)}, u32[]{:S(2)}) collective-permute-start(bf16[2,768,1024]{2,1,0:T(8,128)(2,1)} %dynamic-slice_bitcast_fusion.3), channel_id=1, source_target_pairs={{0,16},{4,20},{8,24},{12,28},{16,0},{20,4},{24,8},{28,12},{1,17},{... | collective-permute-start | bytes 9437192 | tf_op jit(solution)/shard_map/ppermute | solution.py:555
  1019.6 115.5 %collective-permute-start.22 = (bf16[2,768,1024]{2,1,0:T(8,128)(2,1)}, bf16[2,768,1024]{2,1,0:T(8,128)(2,1)}, u32[]{:S(2)}, u32[]{:S(2)}) collective-permute-start(bf16[2,768,1024]{2,1,0:T(8,128)(2,1)} %dynamic-slice_bitcast_fusion.4), channel_id=1, source_target_pairs={{0,8},{4,12},{8,0},{12,4},{16,24},{20,28},{24,16},{28,20},{1,9},{5... | collective-permute-start | bytes 9437192 | tf_op jit(solution)/shard_map/ppermute | solution.py:555
  1069.2 71.8 %collective-permute-start.30 = (bf16[768,1152]{1,0:T(8,128)(2,1)}, bf16[768,1152]{1,0:T(8,128)(2,1)}, u32[]{:S(2)}, u32[]{:S(2)}) collective-permute-start(bf16[768,1152]{1,0:T(8,128)(2,1)} %dynamic-slice_bitcast_fusion.6), channel_id=1, source_target_pairs={{0,8},{4,12},{8,0},{12,4},{16,24},{20,28},{24,16},{28,20},{1,9},{5... | collective-permute-start | bytes 5308424 | tf_op jit(solution)/shard_map/ppermute | solution.py:555
  1133.5 51.8 %collective-permute-start.25 = (bf16[768,1024]{1,0:T(8,128)(2,1)S(1)}, bf16[768,1024]{1,0:T(8,128)(2,1)S(1)}, u32[]{:S(2)}, u32[]{:S(2)}) collective-permute-start(bf16[768,1024]{1,0:T(8,128)(2,1)S(1)} %dynamic-slice_bitcast_fusion.7), channel_id=1, source_target_pairs={{0,8},{4,12},{8,0},{12,4},{16,24},{20,28},{24,16},{28,20},{1,9},{5... | collective-permute-start | bytes 4718600 | tf_op jit(solution)/shard_map/ppermute | solution.py:555
  1138.8 47.2 %collective-permute-start.23 = (bf16[768,1024]{1,0:T(8,128)(2,1)S(1)}, bf16[768,1024]{1,0:T(8,128)(2,1)S(1)}, u32[]{:S(2)}, u32[]{:S(2)}) collective-permute-start(bf16[768,1024]{1,0:T(8,128)(2,1)S(1)} %dynamic-slice_bitcast_fusion.8), channel_id=1, source_target_pairs={{0,16},{4,20},{8,24},{12,28},{16,0},{20,4},{24,8},{28,12},{1,17},{... | collective-permute-start | bytes 4718600 | tf_op jit(solution)/shard_map/ppermute | solution.py:555
  1143.3 74.0 %collective-permute-start.31 = (bf16[192,2176]{1,0:T(8,128)(2,1)S(1)}, bf16[192,2176]{1,0:T(8,128)(2,1)S(1)}, u32[]{:S(2)}, u32[]{:S(2)}) collective-permute-start(bf16[192,2176]{1,0:T(8,128)(2,1)S(1)} %get-tuple-element.76), channel_id=1, source_target_pairs={{0,1},{1,2},{2,3},{3,0},{4,5},{5,6},{6,7},{7,4},{8,9},{9,10},{10,1... | collective-permute-start | bytes 2506760 | tf_op jit(solution)/shard_map/ppermute | solution.py:509
  1181.8 58.3 %collective-permute-start.32 = (bf16[192,2176]{1,0:T(8,128)(2,1)S(1)}, bf16[192,2176]{1,0:T(8,128)(2,1)S(1)}, u32[]{:S(2)}, u32[]{:S(2)}) collective-permute-start(bf16[192,2176]{1,0:T(8,128)(2,1)S(1)} %get-tuple-element.77), channel_id=1, source_target_pairs={{0,2},{1,3},{2,0},{3,1},{4,6},{5,7},{6,4},{7,5},{8,10},{9,11},{10,... | collective-permute-start | bytes 2506760 | tf_op jit(solution)/shard_map/ppermute | solution.py:509
  1185.2 54.9 %collective-permute-start.33 = (bf16[192,2176]{1,0:T(8,128)(2,1)S(1)}, bf16[192,2176]{1,0:T(8,128)(2,1)S(1)}, u32[]{:S(2)}, u32[]{:S(2)}) collective-permute-start(bf16[192,2176]{1,0:T(8,128)(2,1)S(1)} %get-tuple-element.78), channel_id=1, source_target_pairs={{0,3},{1,0},{2,1},{3,2},{4,7},{5,4},{6,5},{7,6},{8,11},{9,8},{10,9... | collective-permute-start | bytes 2506760 | tf_op jit(solution)/shard_map/ppermute | solution.py:509
  1186.9 70.1 %collective-permute-start.26 = (bf16[192,2048]{1,0:T(8,128)(2,1)S(1)}, bf16[192,2048]{1,0:T(8,128)(2,1)S(1)}, u32[]{:S(2)}, u32[]{:S(2)}) collective-permute-start(bf16[192,2048]{1,0:T(8,128)(2,1)S(1)} %get-tuple-element.82), channel_id=1, source_target_pairs={{0,1},{1,2},{2,3},{3,0},{4,5},{5,6},{6,7},{7,4},{8,9},{9,10},{10,1... | collective-permute-start | bytes 2359304 | tf_op jit(solution)/shard_map/ppermute | solution.py:509
  1213.9 93.0 %collective-permute-start.27 = (bf16[192,2048]{1,0:T(8,128)(2,1)S(1)}, bf16[192,2048]{1,0:T(8,128)(2,1)S(1)}, u32[]{:S(2)}, u32[]{:S(2)}) collective-permute-start(bf16[192,2048]{1,0:T(8,128)(2,1)S(1)} %get-tuple-element.83), channel_id=1, source_target_pairs={{0,2},{1,3},{2,0},{3,1},{4,6},{5,7},{6,4},{7,5},{8,10},{9,11},{10,... | collective-permute-start | bytes 2359304 | tf_op jit(solution)/shard_map/ppermute | solution.py:509
  1217.3 89.6 %collective-permute-start.28 = (bf16[192,2048]{1,0:T(8,128)(2,1)S(1)}, bf16[192,2048]{1,0:T(8,128)(2,1)S(1)}, u32[]{:S(2)}, u32[]{:S(2)}) collective-permute-start(bf16[192,2048]{1,0:T(8,128)(2,1)S(1)} %get-tuple-element.84), channel_id=1, source_target_pairs={{0,3},{1,0},{2,1},{3,2},{4,7},{5,4},{6,5},{7,6},{8,11},{9,8},{10,9... | collective-permute-start | bytes 2359304 | tf_op jit(solution)/shard_map/ppermute | solution.py:509
  1309.4 407.0 %reduce-scatter.10.cloned.1.call-start = ((), (), s32[]{:S(2)}) async-start(), calls=%async_computation.9 | async-start | bytes 1081344
  1426.5 330.6 %reduce-scatter.8.cloned.1.call-start = ((), (), s32[]{:S(2)}) async-start(), calls=%async_computation.8 | async-start | bytes 2359296 | tf_op jit(solution)/shard_map/reduce_scatter | solution.py:758
  1431.9 390.4 %reduce-scatter.6.cloned.1.call-start = ((), (), s32[]{:S(2)}) async-start(), calls=%async_computation.7 | async-start | bytes 7077888 | tf_op jit(solution)/shard_map/reduce_scatter | solution.py:764
  1441.4 30.0 %collective-permute-start.44 = (bf16[4,256,512]{2,1,0:T(8,128)(2,1)}, bf16[4,256,512]{2,1,0:T(8,128)(2,1)}, u32[]{:S(2)}, u32[]{:S(2)}) collective-permute-start(bf16[4,256,512]{2,1,0:T(8,128)(2,1)} %get-tuple-element.58), channel_id=1, source_target_pairs={{0,1},{1,2},{2,3},{3,0},{4,5},{5,6},{6,7},{7,4},{8,9},{9,10},{10,1... | collective-permute-start | bytes 3145736 | tf_op jit(solution)/shard_map/ppermute | solution.py:509
  1441.5 75.6 %collective-permute-start.45 = (bf16[4,256,512]{2,1,0:T(8,128)(2,1)}, bf16[4,256,512]{2,1,0:T(8,128)(2,1)S(1)}, u32[]{:S(2)}, u32[]{:S(2)}) collective-permute-start(bf16[4,256,512]{2,1,0:T(8,128)(2,1)} %get-tuple-element.59), channel_id=1, source_target_pairs={{0,2},{1,3},{2,0},{3,1},{4,6},{5,7},{6,4},{7,5},{8,10},{9,11},{10,... | collective-permute-start | bytes 3145736 | tf_op jit(solution)/shard_map/ppermute | solution.py:509
  1442.8 112.6 %collective-permute-start.46 = (bf16[4,256,512]{2,1,0:T(8,128)(2,1)}, bf16[4,256,512]{2,1,0:T(8,128)(2,1)S(1)}, u32[]{:S(2)}, u32[]{:S(2)}) collective-permute-start(bf16[4,256,512]{2,1,0:T(8,128)(2,1)} %get-tuple-element.60), channel_id=1, source_target_pairs={{0,3},{1,0},{2,1},{3,2},{4,7},{5,4},{6,5},{7,6},{8,11},{9,8},{10,9... | collective-permute-start | bytes 3145736 | tf_op jit(solution)/shard_map/ppermute | solution.py:509
  1445.5 142.7 %collective-permute-start.41 = (bf16[4,256,512]{2,1,0:T(8,128)(2,1)}, bf16[4,256,512]{2,1,0:T(8,128)(2,1)S(1)}, u32[]{:S(2)}, u32[]{:S(2)}) collective-permute-start(bf16[4,256,512]{2,1,0:T(8,128)(2,1)} %get-tuple-element.54), channel_id=1, source_target_pairs={{0,1},{1,2},{2,3},{3,0},{4,5},{5,6},{6,7},{7,4},{8,9},{9,10},{10,1... | collective-permute-start | bytes 3145736 | tf_op jit(solution)/shard_map/ppermute | solution.py:509
  1445.9 200.6 %collective-permute-start.42 = (bf16[4,256,512]{2,1,0:T(8,128)(2,1)}, bf16[4,256,512]{2,1,0:T(8,128)(2,1)}, u32[]{:S(2)}, u32[]{:S(2)}) collective-permute-start(bf16[4,256,512]{2,1,0:T(8,128)(2,1)} %get-tuple-element.55), channel_id=1, source_target_pairs={{0,2},{1,3},{2,0},{3,1},{4,6},{5,7},{6,4},{7,5},{8,10},{9,11},{10,... | collective-permute-start | bytes 3145736 | tf_op jit(solution)/shard_map/ppermute | solution.py:509
  1471.5 175.0 %collective-permute-start.43 = (bf16[4,256,512]{2,1,0:T(8,128)(2,1)}, bf16[4,256,512]{2,1,0:T(8,128)(2,1)}, u32[]{:S(2)}, u32[]{:S(2)}) collective-permute-start(bf16[4,256,512]{2,1,0:T(8,128)(2,1)} %get-tuple-element.56), channel_id=1, source_target_pairs={{0,3},{1,0},{2,1},{3,2},{4,7},{5,4},{6,5},{7,6},{8,11},{9,8},{10,9... | collective-permute-start | bytes 3145736 | tf_op jit(solution)/shard_map/ppermute | solution.py:509
  1517.1 140.7 %collective-permute-start.34 = (bf16[192,2048]{1,0:T(8,128)(2,1)}, bf16[192,2048]{1,0:T(8,128)(2,1)S(1)}, u32[]{:S(2)}, u32[]{:S(2)}) collective-permute-start(bf16[192,2048]{1,0:T(8,128)(2,1)} %get-tuple-element.79), channel_id=1, source_target_pairs={{0,1},{1,2},{2,3},{3,0},{4,5},{5,6},{6,7},{7,4},{8,9},{9,10},{10,1... | collective-permute-start | bytes 2359304 | tf_op jit(solution)/shard_map/ppermute | solution.py:509
  1555.4 138.5 %collective-permute-start.35 = (bf16[192,2048]{1,0:T(8,128)(2,1)}, bf16[192,2048]{1,0:T(8,128)(2,1)S(1)}, u32[]{:S(2)}, u32[]{:S(2)}) collective-permute-start(bf16[192,2048]{1,0:T(8,128)(2,1)} %get-tuple-element.81), channel_id=1, source_target_pairs={{0,2},{1,3},{2,0},{3,1},{4,6},{5,7},{6,4},{7,5},{8,10},{9,11},{10,... | collective-permute-start | bytes 2359304 | tf_op jit(solution)/shard_map/ppermute | solution.py:509
  1589.2 104.7 %collective-permute-start.36 = (bf16[192,2048]{1,0:T(8,128)(2,1)}, bf16[192,2048]{1,0:T(8,128)(2,1)S(1)}, u32[]{:S(2)}, u32[]{:S(2)}) collective-permute-start(bf16[192,2048]{1,0:T(8,128)(2,1)} %get-tuple-element.80), channel_id=1, source_target_pairs={{0,3},{1,0},{2,1},{3,2},{4,7},{5,4},{6,5},{7,6},{8,11},{9,8},{10,9... | collective-permute-start | bytes 2359304 | tf_op jit(solution)/shard_map/ppermute | solution.py:509
  1757.1 70.1 %collective-permute-start.40 = (bf16[64,2048]{1,0:T(8,128)(2,1)}, bf16[64,2048]{1,0:T(8,128)(2,1)S(1)}, u32[]{:S(2)}, u32[]{:S(2)}) collective-permute-start(bf16[64,2048]{1,0:T(8,128)(2,1)} %reduce-scatter.8.cloned.1.call-done), channel_id=1, source_target_pairs={{0,0},{1,8},{2,16},{3,24},{4,1},{5,9},{6,17},{7,25},{8,2},{9,10},{... | collective-permute-start | bytes 786440 | tf_op jit(solution)/shard_map/ppermute | solution.py:759
  (75 other events, 1903.1 us)
Sparse Core Ops, SparseCore 0:
  9.6 80.6 all-gather.4
  93.1 221.1 all-gather.8
  317.7 295.1 all-gather.6
  1309.5 77.1 all-gather.10
  1426.6 289.7 reduce-scatter.9
  1719.6 37.4 reduce-scatter.7
  1760.5 61.7 reduce-scatter.5

commit v2 on v1

--- a/solution.py
+++ b/solution.py
@@ -231,9 +231,9 @@
     refs = refs[4:]
     gate_refs, up_refs, wd_ref = refs[:shards], refs[shards : 2 * shards], refs[2 * shards]
     refs = refs[2 * shards + 1 :]
-    out_hbm, dx_hbm, dwd_hbm = refs[:3]
-    dwg_hbm, dwu_hbm = refs[3 : 3 + shards], refs[3 + shards : 3 + 2 * shards]
-    refs = refs[3 + 2 * shards :]
+    out_hbm, dx_kept, dx_sent, dwd_hbm = refs[:4]
+    dwg_hbm, dwu_hbm = refs[4 : 4 + shards], refs[4 + shards : 4 + 2 * shards]
+    refs = refs[4 + 2 * shards :]
     x_slots, g_slots, gates_col, acc_g, acc_u, acc_d, out_stage, dx_stage = refs[:8]
     out_sem, dx_sem, acc_sem, grad_sem = refs[8:]
     b = pl.program_id(0)
@@ -347,13 +347,26 @@
                 dx_stage[slot, :, cols] = mm(select, ds_, TN).astype(low_type)
             tail = jnp.concatenate([g_slots[j, part, width:] for j in range(locals_)], axis=0)
             dx_stage[slot, :, width:] = mm(select, tail, TN).astype(low_type)
-            at = pl.ds((b * sources + s) * rows, rows)
+            number = b * sources + s
+            group = lax.div(number, shards)
+            within = number - group * shards
+            at = pl.ds(number * rows, rows)
+            to = pl.ds((lax.div(group, 2) * shards + within) * rows, rows)
             copies = (
                 pltpu.make_async_copy(out_stage.at[slot], out_hbm.at[at], out_sem.at[slot]),
-                pltpu.make_async_copy(dx_stage.at[slot], dx_hbm.at[at], dx_sem.at[slot]),
+                pltpu.make_async_copy(dx_stage.at[slot], dx_kept.at[to], dx_sem.at[slot]),
             )
-            for copy in copies:
-                copy.start()
+            copies[0].start()
+            mine_too = lax.rem(group, 2) == place_ref[2]
+
+            @pl.when(mine_too)
+            def _():
+                copies[1].start()
+
+            @pl.when(jnp.logical_not(mine_too))
+            def _():
+                pltpu.make_async_copy(dx_stage.at[slot], dx_sent.at[to], dx_sem.at[slot]).start()
+
             pending[slot] = copies
         for copies in pending:
             if copies is not None:
@@ -404,7 +417,7 @@
             *([weight_spec] * (2 * shards)),
             pl.BlockSpec((1, hidden, width), lambda b, e, *_: (e, 0, 0)),
         ],
-        out_specs=[any_spec] * (3 + 2 * shards),
+        out_specs=[any_spec] * (4 + 2 * shards),
         scratch_shapes=[
             pltpu.VMEM((locals_, held_rows, width), low_type),
             pltpu.VMEM((locals_, held_rows, width + 128), low_type),
@@ -428,7 +441,8 @@
         grid_spec=grid_spec,
         out_shape=[
             jax.ShapeDtypeStruct((tokens_all, width), low_type),
-            jax.ShapeDtypeStruct((tokens_all, width + 128), low_type),
+            jax.ShapeDtypeStruct((tokens_all // 2, width + 128), low_type),
+            jax.ShapeDtypeStruct((tokens_all // 2, width + 128), low_type),
             jax.ShapeDtypeStruct((locals_, hidden, width), jnp.float32),
             *([piece] * (2 * shards)),
         ],
@@ -441,7 +455,7 @@
         ),
         name="experts",
     )(place, x_all, g_all, rank, router_rows, *gate_parts, *up_parts, w_down)
-    return got[0], got[1], got[2], got[3 : 3 + shards], got[3 + shards :]
+    return got[:4], got[4 : 4 + shards], got[4 + shards :]
 
 
 def split_columns(me, weights, shards):
@@ -534,14 +548,14 @@
     return result
 
 
-def fs_sum(partial):
+def fs_sum(partial, after=(), wire=low_type):
     count = lax.axis_size("fs")
-    me = lax.axis_index("fs")
+    me = tied(lax.axis_index("fs"), after)
     rows = partial.shape[0] // count
     own = lax.dynamic_slice_in_dim(partial, me * rows, rows).astype(jnp.float32)
     for step in range(1, count):
         sent = lax.dynamic_slice_in_dim(partial, ((me + step) % count) * rows, rows)
-        own = own + shifted(sent.astype(low_type), count, step).astype(jnp.float32)
+        own = own + shifted(sent.astype(wire), count, step).astype(jnp.float32)
     return own
 
 
@@ -568,35 +582,52 @@
     return held.reshape((1 << bits,) + values.shape)
 
 
-def ep_sum(partial, after=None):
+def tied(number, arrays):
+    for array in arrays:
+        corner = lax.slice(array, (0,) * array.ndim, (1,) * array.ndim)
+        number = number + (jnp.sum(corner.astype(jnp.float32)) * 0.0).astype(jnp.int32)
+    return number
+
+
+def ep_halve(kept, sent, bit):
+    got = ep_flip(sent, bit)
+    return (kept.astype(jnp.float32) + got.astype(jnp.float32)).astype(kept.dtype)
+
+
+def ep_pick(held, bit, axis, me):
+    mine = (me >> bit) & 1
+    return (
+        lax.dynamic_index_in_dim(held, mine, axis, False),
+        lax.dynamic_index_in_dim(held, 1 - mine, axis, False),
+    )
+
+
+def ep_sum(partial, after=()):
     count = lax.axis_size("ep")
-    bits = count.bit_length() - 1
-    me = lax.axis_index("ep")
+    me = tied(lax.axis_index("ep"), after)
     rows, columns = partial.shape[0] // count, partial.shape[1]
-
-    if after is not None:
-        me = me + (after[0, 0].astype(jnp.float32) * 0.0).astype(jnp.int32)
-
-    def halve(held, bit, axis):
-        mine = (me >> bit) & 1
-        got = ep_flip(lax.dynamic_index_in_dim(held, 1 - mine, axis, False), bit)
-        kept = lax.dynamic_index_in_dim(held, mine, axis, False)
-        return (kept.astype(jnp.float32) + got.astype(jnp.float32)).astype(low_type)
-
-    first = halve(partial.reshape(count // 2, 2, rows, columns), 0, 1)
+    kept, sent = ep_pick(partial.reshape(count // 2, 2, rows, columns), 0, 1, me)
+    return ep_rest(ep_halve(kept, sent, 0), me)
+
+
+def ep_rest(first, me):
+    bits = lax.axis_size("ep").bit_length() - 1
+    rows, columns = first.shape[1:]
     half = columns // 2 // 128 * 128
     results = []
     for start, stop, order in (
         (0, half, range(1, bits)),
         (half, columns, range(bits - 1, 0, -1)),
     ):
+        if start == stop:
+            continue
         held = first[:, :, start:stop].reshape((2,) * (bits - 1) + (rows, stop - start))
         left = list(range(bits - 1, 0, -1))
         for bit in order:
-            held = halve(held, bit, left.index(bit))
+            held = ep_halve(*ep_pick(held, bit, left.index(bit), me), bit)
             left.remove(bit)
         results.append(held)
-    return jnp.concatenate(results, axis=1)
+    return jnp.concatenate(results, axis=1) if len(results) > 1 else results[0]
 
 
 def on_device(
@@ -701,7 +732,9 @@
     normed_group = (group_in * group_scale * gain_one).astype(low_type)
     qkv = mm(normed_group, w_heads, NN)
     attended = attention_forward(qkv, gain_query, gain_key, cos2, sin2, segment, head_dim)
-    branch = fs_sum(mm(attended, w_output, NN).astype(low_type))
+    branch = fs_sum(
+        mm(attended, w_output, NN).astype(low_type), (*gate_parts[1:], *up_parts[1:])
+    )
     hidden_in = tokens.astype(jnp.float32)
     scale_one = rms_scale(hidden_in)
     hidden_mid = hidden_in + branch
@@ -709,8 +742,8 @@
     normed_two = (hidden_mid * scale_two * gain_two).astype(low_type)
 
     normed_all = lax.all_gather(normed_two, ("ep", "fs"), axis=0, tiled=True)
-    out_part, dx_part, dwd, dwg, dwu = run_experts(
-        jnp.stack([base, fs_at]).astype(jnp.int32),
+    (out_part, dx_kept, dx_sent, dwd), dwg, dwu = run_experts(
+        jnp.stack([base, fs_at, ep_at & 1]).astype(jnp.int32),
         normed_all,
         grad_all,
         rank_rolled,
@@ -720,10 +753,12 @@
         w_down,
         capacity,
     )
-    dx_group = ep_sum(dx_part)
-    dx_own = fs_sum(dx_group)
-    gate_grad = join_columns(fs_place, fs_send(dwg))
-    up_grad = join_columns(fs_place, fs_send(dwu))
+    dwg = fs_send(dwg)
+    dwu = fs_send(dwu)
+    dx_first = ep_halve(dx_kept, dx_sent, 0).reshape(n_ep // 2, group_rows, dx_kept.shape[1])
+    dx_own = fs_sum(ep_rest(dx_first, ep_at), (*dwg[1:], *dwu[1:]))
+    gate_grad = join_columns(fs_place, dwg)
+    up_grad = join_columns(fs_place, dwu)
 
     logits = mm(normed_two, router_full, NN)
     kept = jnp.where(hit, logits, -1e30)
@@ -784,11 +819,12 @@
         axis=1,
     )
     sums = jnp.pad(sums, ((0, 0), (0, 128 - sums.shape[1])))
-    sums = lax.psum_scatter(sums, ("ep", "fs"), scatter_dimension=0, tiled=True)
+    sums = fs_sum(ep_sum(sums), wire=jnp.float32)
     each = head_dim // devices
 
-    out_group = ep_sum(out_part, dx_group)
-    output = (hidden_mid + fs_sum(out_group)).astype(low_type)
+    out_group = ep_sum(out_part, (dx_own,))
+    mixed = lax.psum_scatter(out_group, "fs", scatter_dimension=0, tiled=True)
+    output = (hidden_mid + mixed.astype(jnp.float32)).astype(low_type)
     return (
         output,
         tokens_grad,

time: 1860 us -> 1710 us (0.919)
  starting transfers between devices: 258 us -> 159 us
  waiting for transfers between devices: 1090 us -> 1030 us
    all_gather x1, waiting for transfers between devices: 17.7 us -> 164 us  [on_device(): normed_all = lax.all_gather(normed_two, ('ep', 'fs'), axis=0, tiled=True)]
    ppermute x33, waiting for transfers between devices: 595 us -> 472 us  [shifted(): lax.ppermute(values, 'fs', [(i, (i + step) % count) for i in range(count)])]
    ppermute x33, starting transfers between devices: 240 us -> 142 us  [shifted(): lax.ppermute(values, 'fs', [(i, (i + step) % count) for i in range(count)])]
    reduce_scatter x0 -> x1, waiting for transfers between devices: none -> 68.5 us  [on_device(): mixed = lax.psum_scatter(out_group, 'fs', scatter_dimension=0, tiled=True)]
    reduce_scatter x1, waiting for transfers between devices: 63.6 us -> 0.01 us  [on_device(): lax.psum_scatter(heads_w_grad, 'ep', scatter_dimension=0, tiled=True)]
    reduce_scatter x1, waiting for transfers between devices: 37.1 us -> 0.01 us  [on_device(): lax.psum_scatter(output_w_grad, 'ep', scatter_dimension=0, tiled=True)]
    ppermute x13 -> x16, waiting for transfers between devices: 286 us -> 257 us  [ep_flip(): return lax.ppermute(values, 'ep', [(i, i ^ 1 << bit) for i in range(count)])]
    squeeze x10 -> x12, local copies, waits for them, and re-layouts: 38.5 us -> 28.4 us  [the longest x10 27.4 us: ep_pick(): lax.dynamic_index_in_dim(held, 1 - mine, axis, False)]
  transfers between devices with their start and end apart: 54 -> 57, of which waited for: 32 -> 30; matrix products, arithmetic and copies ran while one was open for 8% -> 9% of each run, Pallas kernels for 2% -> 4%
where the time goes in v2:
time: 1710 us; the launch traced here: 1700 us
  waiting for transfers between devices  1030 us (60%)
  Pallas kernels  243 us (14%)
  starting transfers between devices  159 us (9%)
  local copies, waits for them, and re-layouts  124 us (7%)
  other arithmetic  87.1 us (5%)
  matrix products  38.6 us (2%)
  between operations  24.6 us (1%)
    ppermute x33, waiting for transfers between devices, shifted(): lax.ppermute(values, 'fs', [(i, (i + step) % count) for i in range(count)])  472 us
    ppermute x16, waiting for transfers between devices, ep_flip(): return lax.ppermute(values, 'ep', [(i, i ^ 1 << bit) for i in range(count)])  257 us
    pallas_call x1, Pallas kernels, run_experts(): pl.pallas_call(lambda *refs: experts_kernel(*refs, sources=sources, cap=c...  183 us
    all_gather x1, waiting for transfers between devices, on_device(): normed_all = lax.all_gather(normed_two, ('ep', 'fs'), axis=0, tiled=True)  164 us
    ppermute x33, starting transfers between devices, shifted(): lax.ppermute(values, 'fs', [(i, (i + step) % count) for i in range(count)])  142 us
    reduce_scatter x1, waiting for transfers between devices, on_device(): mixed = lax.psum_scatter(out_group, 'fs', scatter_dimension=0, tiled=True)  68.5 us
    all_gather x1, waiting for transfers between devices, on_device(): lax.all_gather(grad_mid.astype(low_type), 'fs', axis=0, tiled=True)  63.4 us
    convert_element_type x10, other arithmetic, ep_halve(): (kept.astype(jnp.float32) + got.astype(jnp.float32)).astype(kept.dtype)  42.3 us
  transfers between devices with their start and end apart: 57, of which 30 were waited for; matrix products, arithmetic and copies ran while one was open for 9% of the time, Pallas kernels for 4%

profile of v2, /device:TPU:0, one launch (start us, length us, event | category | flops | bytes accessed | tf_op | source)
XLA Modules:
  0.0 1702.3 jit_solution(14552825234347445551)
XLA Ops:
  23.8 6.1 collective-permute-done.3
  30.0 15.6 collective-permute-done.4
  47.3 17.5 %collective-permute-done.6 = bf16[4,64,3,512]{3,1,2,0:T(8,128)(2,1)S(1)} collective-permute-done((bf16[4,64,3,512]{3,1,2,0:T(8,128)(2,1)S(1)}, bf16[4,64,3,512]{3,1,2,0:T(8,128)(2,1)S(1)}, u32[]{:S(2)}, u32[]{:S(2)}) %collective-permute-start.6) | collective-permute-done | bytes 786464 | tf_op jit(solution)/shard_map/ppermute | solution.py:569
  66.8 33.7 %collective-permute-done.7 = bf16[2,4,64,3,512]{4,2,3,1,0:T(8,128)(2,1)} collective-permute-done((bf16[2,4,64,3,512]{4,2,3,1,0:T(8,128)(2,1)S(1)}, bf16[2,4,64,3,512]{4,2,3,1,0:T(8,128)(2,1)}, u32[]{:S(2)}, u32[]{:S(2)}) %collective-permute-start.7) | collective-permute-done | bytes 1572896 | tf_op jit(solution)/shard_map/ppermute | solution.py:569
  104.7 7.1 split_columns.1
  111.7 21.3 %collective-permute-start.9 = (bf16[4,512,256]{2,1,0:T(8,128)(2,1)}, bf16[4,512,256]{2,1,0:T(8,128)(2,1)}, u32[]{:S(2)}, u32[]{:S(2)}) collective-permute-start(bf16[4,512,256]{2,1,0:T(8,128)(2,1)} %get-tuple-element.39), channel_id=1, source_target_pairs={{0,1},{1,2},{2,3},{3,0},{4,5},{5,6},{6,7},{7,4},{8,9},{9,10},{10,1... | collective-permute-start | bytes 3145736 | tf_op jit(solution)/shard_map/ppermute | solution.py:523
  136.9 47.1 %collective-permute-done = bf16[17472]{0:T(1024)(128)(2,1)S(1)} collective-permute-done((bf16[17472]{0:T(1024)(128)(2,1)S(1)}, bf16[17472]{0:T(1024)(128)(2,1)S(1)}, u32[]{:S(2)}, u32[]{:S(2)}) %collective-permute-start) | collective-permute-done | bytes 34976 | tf_op jit(solution)/shard_map/ppermute | solution.py:523
  185.6 43.4 %collective-permute-done.1 = bf16[17472]{0:T(1024)(128)(2,1)S(1)} collective-permute-done((bf16[17472]{0:T(1024)(128)(2,1)S(1)}, bf16[17472]{0:T(1024)(128)(2,1)S(1)}, u32[]{:S(2)}, u32[]{:S(2)}) %collective-permute-start.1) | collective-permute-done | bytes 34976 | tf_op jit(solution)/shard_map/ppermute | solution.py:523
  229.0 16.2 collective-permute-start.11
  258.6 71.3 %collective-permute-done.11.refs_8_ = bf16[4,512,256]{2,1,0:T(8,128)(2,1)} collective-permute-done((bf16[4,512,256]{2,1,0:T(8,128)(2,1)}, bf16[4,512,256]{2,1,0:T(8,128)(2,1)}, u32[]{:S(2)}, u32[]{:S(2)}) %collective-permute-start.11) | collective-permute-done | bytes 1048608 | tf_op jit(solution)/shard_map/ppermute | solution.py:523
  331.7 4.9 collective-permute-done.12.refs_10_
  338.4 68.4 %collective-permute-done.13.refs_11_ = bf16[4,512,256]{2,1,0:T(8,128)(2,1)} collective-permute-done((bf16[4,512,256]{2,1,0:T(8,128)(2,1)}, bf16[4,512,256]{2,1,0:T(8,128)(2,1)}, u32[]{:S(2)}, u32[]{:S(2)}) %collective-permute-start.13) | collective-permute-done | bytes 1048608 | tf_op jit(solution)/shard_map/ppermute | solution.py:523
  419.2 12.1 copy.80
  431.3 6.2 copy.113
  437.6 5.2 fusion.26.refs_0_.refs_1_.refs_2_
  442.9 12.2 attn_forward.1
  459.4 20.8 %collective-permute-start.15 = (bf16[192,2048]{1,0:T(8,128)(2,1)}, bf16[192,2048]{1,0:T(8,128)(2,1)S(1)}, u32[]{:S(2)}, u32[]{:S(2)}) collective-permute-start(bf16[192,2048]{1,0:T(8,128)(2,1)} %get-tuple-element.84), channel_id=1, source_target_pairs={{0,1},{1,2},{2,3},{3,0},{4,5},{5,6},{6,7},{7,4},{8,9},{9,10},{10,1... | collective-permute-start | bytes 2359304 | tf_op jit(solution)/shard_map/ppermute | solution.py:523
  483.6 18.2 %collective-permute-done.15 = bf16[192,2048]{1,0:T(8,128)(2,1)S(1)} collective-permute-done((bf16[192,2048]{1,0:T(8,128)(2,1)}, bf16[192,2048]{1,0:T(8,128)(2,1)S(1)}, u32[]{:S(2)}, u32[]{:S(2)}) %collective-permute-start.15) | collective-permute-done | bytes 786464 | tf_op jit(solution)/shard_map/ppermute | solution.py:523
  501.7 32.9 %collective-permute-done.16 = bf16[192,2048]{1,0:T(8,128)(2,1)S(1)} collective-permute-done((bf16[192,2048]{1,0:T(8,128)(2,1)}, bf16[192,2048]{1,0:T(8,128)(2,1)S(1)}, u32[]{:S(2)}, u32[]{:S(2)}) %collective-permute-start.16) | collective-permute-done | bytes 786464 | tf_op jit(solution)/shard_map/ppermute | solution.py:523
  544.3 163.8 %all-gather.7.cloned.1.call-done.refs_1_ = bf16[6144,2048]{1,0:T(8,128)(2,1)} async-done(((bf16[192,2048]{1,0:T(8,128)(2,1)}), bf16[6144,2048]{1,0:T(8,128)(2,1)}) %all-gather.7.cloned.1.call-update) | async-done | bytes 25165840 | tf_op jit(solution)/shard_map/all_gather | solution.py:744
  708.1 182.6 %experts.1 = (bf16[6144,2048]{1,0:T(8,128)(2,1)}, bf16[3072,2176]{1,0:T(8,128)(2,1)}, bf16[3072,2176]{1,0:T(8,128)(2,1)}, f32[4,256,2048]{2,1,0:T(8,128)}, bf16[...) custom-call(s32[3]{0:T(128)} %pad_add_fusion.refs_0_, ...), custom_call_target="tpu_custom_call", output_to_operand_aliasing={{0}: (1, {})} | custom-call | flops 77309411328 | bytes 100663296 | tf_op jit(solution)/shard_map/experts/pallas_call | solution.py:437
  891.1 20.3 %collective-permute-done.18 = bf16[3072,2176]{1,0:T(8,128)(2,1)} collective-permute-done((bf16[3072,2176]{1,0:T(8,128)(2,1)}, bf16[3072,2176]{1,0:T(8,128)(2,1)}, u32[]{:S(2)}, u32[]{:S(2)}) %collective-permute-start.18) | collective-permute-done | bytes 13369376 | tf_op jit(solution)/shard_map/ppermute | solution.py:569
  911.4 10.4 add_convert_fusion
  943.4 60.0 %collective-permute-done.19 = bf16[2,768,1024]{2,1,0:T(8,128)(2,1)} collective-permute-done((bf16[2,768,1024]{2,1,0:T(8,128)(2,1)}, bf16[2,768,1024]{2,1,0:T(8,128)(2,1)}, u32[]{:S(2)}, u32[]{:S(2)}) %collective-permute-start.19) | collective-permute-done | bytes 3145760 | tf_op jit(solution)/shard_map/ppermute | solution.py:569
  1010.7 7.4 collective-permute-done.21
  1025.6 9.6 collective-permute-start.28
  1040.0 11.6 collective-permute-done.26.refs_1_
  1052.9 48.1 %collective-permute-done.27.refs_2_ = bf16[4,256,512]{2,1,0:T(8,128)(2,1)} collective-permute-done((bf16[4,256,512]{2,1,0:T(8,128)(2,1)}, bf16[4,256,512]{2,1,0:T(8,128)(2,1)}, u32[]{:S(2)}, u32[]{:S(2)}) %collective-permute-start.27) | collective-permute-done | bytes 1048608 | tf_op jit(solution)/shard_map/ppermute | solution.py:523
  1102.7 19.5 %collective-permute-done.28.refs_3_ = bf16[4,256,512]{2,1,0:T(8,128)(2,1)} collective-permute-done((bf16[4,256,512]{2,1,0:T(8,128)(2,1)}, bf16[4,256,512]{2,1,0:T(8,128)(2,1)}, u32[]{:S(2)}, u32[]{:S(2)}) %collective-permute-start.28) | collective-permute-done | bytes 1048608 | tf_op jit(solution)/shard_map/ppermute | solution.py:523
  1134.6 19.7 %collective-permute-done.29 = bf16[192,2176]{1,0:T(8,128)(2,1)} collective-permute-done((bf16[192,2176]{1,0:T(8,128)(2,1)}, bf16[192,2176]{1,0:T(8,128)(2,1)}, u32[]{:S(2)}, u32[]{:S(2)}) %collective-permute-start.29) | collective-permute-done | bytes 835616 | tf_op jit(solution)/shard_map/ppermute | solution.py:523
  1154.3 34.8 %collective-permute-done.30 = bf16[192,2176]{1,0:T(8,128)(2,1)} collective-permute-done((bf16[192,2176]{1,0:T(8,128)(2,1)}, bf16[192,2176]{1,0:T(8,128)(2,1)}, u32[]{:S(2)}, u32[]{:S(2)}) %collective-permute-start.30) | collective-permute-done | bytes 835616 | tf_op jit(solution)/shard_map/ppermute | solution.py:523
  1193.5 11.2 dynamic-slice_bitcast_fusion
  1204.8 19.5 %collective-permute-done.32 = bf16[4,768,2048]{2,1,0:T(8,128)(2,1)} collective-permute-done((bf16[4,768,2048]{2,1,0:T(8,128)(2,1)}, bf16[4,768,2048]{2,1,0:T(8,128)(2,1)}, u32[]{:S(2)}, u32[]{:S(2)}) %collective-permute-start.32) | collective-permute-done | bytes 12582944 | tf_op jit(solution)/shard_map/ppermute | solution.py:569
  1224.3 10.8 fusion
  1248.3 64.4 %collective-permute-done.33 = bf16[2,768,1024]{2,1,0:T(8,128)(2,1)} collective-permute-done((bf16[2,768,1024]{2,1,0:T(8,128)(2,1)}, bf16[2,768,1024]{2,1,0:T(8,128)(2,1)}, u32[]{:S(2)}, u32[]{:S(2)}) %collective-permute-start.33) | collective-permute-done | bytes 3145760 | tf_op jit(solution)/shard_map/ppermute | solution.py:569
  1323.0 29.9 %collective-permute-done.34 = bf16[768,1024]{1,0:T(8,128)(2,1)S(1)} collective-permute-done((bf16[768,1024]{1,0:T(8,128)(2,1)S(1)}, bf16[768,1024]{1,0:T(8,128)(2,1)S(1)}, u32[]{:S(2)}, u32[]{:S(2)}) %collective-permute-start.34) | collective-permute-done | bytes 1572896 | tf_op jit(solution)/shard_map/ppermute | solution.py:569
  1366.8 68.5 %reduce-scatter.4.cloned.1.call-done = bf16[192,2048]{1,0:T(8,128)(2,1)} async-done(((bf16[768,2048]{1,0:T(8,128)(2,1)}), bf16[192,2048]{1,0:T(8,128)(2,1)}) %reduce-scatter.4.cloned.1.call-update) | async-done | bytes 786448 | tf_op jit(solution)/shard_map/reduce_scatter | solution.py:826
  1440.1 63.4 %all-gather.11.cloned.1.call-done = bf16[768,2048]{1,0:T(8,128)(2,1)} async-done(((bf16[192,2048]{1,0:T(8,128)(2,1)}), bf16[768,2048]{1,0:T(8,128)(2,1)}) %all-gather.11.cloned.1.call-update) | async-done | bytes 3145744 | tf_op jit(solution)/shard_map/all_gather | solution.py:779
  1503.5 5.1 convolution_convert_fusion.2
  1516.1 18.4 %attn_backward.1 = (bf16[768,512]{1,0:T(8,128)(2,1)S(1)}, bf16[768,512]{1,0:T(8,128)(2,1)S(1)}, bf16[768,512]{1,0:T(8,128)(2,1)S(1)}, f32[4,1,128]{2,1,0:T(1,128)S(1)}, f32[4,1,128]{2,1,0:T(1,128)S(1)}) custom-call(f32[768,1536]{1,0:T(8,128)S(1)} %copy-done.1, f32[768,1536]{1,0:T(8,128)S(1)} %copy-done.1, f32[768,1536]{1,0:T(8,128)S(1)} %copy-done.1, ...), custom_call_target="tpu_custom_call" | custom-call | flops 3019898880 | bytes 7077888 | tf_op jit(solution)/shard_map/attn_backward/pallas_call | solution.py:196
  1537.2 7.5 convolution_convert_fusion
  1547.3 8.6 fusion.6
  1578.4 11.3 join_columns.3
  1589.7 11.4 join_columns.2
  1604.7 21.2 %collective-permute-done.38 = bf16[192,2048]{1,0:T(8,128)(2,1)} collective-permute-done((bf16[192,2048]{1,0:T(8,128)(2,1)}, bf16[192,2048]{1,0:T(8,128)(2,1)}, u32[]{:S(2)}, u32[]{:S(2)}) %collective-permute-start.38) | collective-permute-done | bytes 786464 | tf_op jit(solution)/shard_map/ppermute | solution.py:523
  1628.5 17.0 collective-permute-start.43
  1660.6 19.3 %collective-permute-start.47 = (bf16[64,1536]{1,0:T(8,128)(2,1)S(1)}, bf16[64,1536]{1,0:T(8,128)(2,1)S(1)}, u32[]{:S(2)}, u32[]{:S(2)}) collective-permute-start(bf16[64,1536]{1,0:T(8,128)(2,1)S(1)} %get-tuple-element.98), channel_id=1, source_target_pairs={{0,2},{1,3},{2,0},{3,1},{4,6},{5,7},{6,4},{7,5},{8,10},{9,11},{10,... | collective-permute-start | bytes 589832 | tf_op jit(solution)/shard_map/ppermute | solution.py:523
  1680.0 5.7 collective-permute-done.47
  (387 shorter events, 236.3 us)
Async XLA Ops:
  7.2 403.4 %all-gather.5.cloned.1.call-start = ((), (), s32[]{:S(2)}) async-start(), calls=%async_computation.3 | async-start | bytes 3932160 | tf_op jit(solution)/shard_map/all_gather | solution.py:668
  7.9 532.8 %all-gather.9.cloned.1.call-start = ((), (), s32[]{:S(2)}) async-start(), calls=%async_computation.5 | async-start | bytes 27574272 | tf_op jit(solution)/shard_map/all_gather | solution.py:709
  11.8 696.3 %all-gather.7.cloned.1.call-start = ((), (), s32[]{:S(2)}) async-start(), calls=%async_computation.4 | async-start | bytes 25952256 | tf_op jit(solution)/shard_map/all_gather | solution.py:744
  19.6 26.0 %collective-permute-start.4 = (bf16[64,3,512]{2,0,1:T(8,128)(2,1)S(1)}, bf16[64,3,512]{2,0,1:T(8,128)(2,1)S(1)}, u32[]{:S(2)}, u32[]{:S(2)}) collective-permute-start(bf16[64,3,512]{2,0,1:T(8,128)(2,1)S(1)} %bitcast.228), channel_id=1, source_target_pairs={{0,2},{1,3},{2,0},{3,1},{4,6},{5,7},{6,4},{7,5},{8,10},{9,11},{10,... | collective-permute-start | bytes 589832 | tf_op jit(solution)/shard_map/ppermute | solution.py:523
  22.3 23.3 %collective-permute-start.5 = (bf16[64,3,512]{2,0,1:T(8,128)(2,1)S(1)}, bf16[64,3,512]{2,0,1:T(8,128)(2,1)S(1)}, u32[]{:S(2)}, u32[]{:S(2)}) collective-permute-start(bf16[64,3,512]{2,0,1:T(8,128)(2,1)S(1)} %bitcast.227), channel_id=1, source_target_pairs={{0,3},{1,0},{2,1},{3,2},{4,7},{5,4},{6,5},{7,6},{8,11},{9,8},{10,9... | collective-permute-start | bytes 589832 | tf_op jit(solution)/shard_map/ppermute | solution.py:523
  65.0 35.5 %collective-permute-start.7 = (bf16[2,4,64,3,512]{4,2,3,1,0:T(8,128)(2,1)S(1)}, bf16[2,4,64,3,512]{4,2,3,1,0:T(8,128)(2,1)}, u32[]{:S(2)}, u32[]{:S(2)}) collective-permute-start(bf16[2,4,64,3,512]{4,2,3,1,0:T(8,128)(2,1)S(1)} %pad_maximum_fusion.3), channel_id=1, source_target_pairs={{0,8},{4,12},{8,0},{12,4},{16,24},{20,28},{24,16},{28,20},{1,9},{5... | collective-permute-start | bytes 4718600 | tf_op jit(solution)/shard_map/ppermute | solution.py:569
  104.6 308.7 %collective-permute-start.8 = (bf16[2,2,4,64,3,512]{5,3,4,2,0,1:T(8,128)(2,1)}, bf16[2,2,4,64,3,512]{5,3,4,2,0,1:T(8,128)(2,1)}, u32[]{:S(2)}, u32[]{:S(2)}) collective-permute-start(bf16[2,2,4,64,3,512]{5,3,4,2,0,1:T(8,128)(2,1)} %pad_maximum_fusion.1), channel_id=1, source_target_pairs={{0,4},{4,0},{8,12},{12,8},{16,20},{20,16},{24,28},{28,24},{1,5},{5... | collective-permute-start | bytes 9437192 | tf_op jit(solution)/shard_map/ppermute | solution.py:569
  111.7 133.4 %collective-permute-start.9 = (bf16[4,512,256]{2,1,0:T(8,128)(2,1)}, bf16[4,512,256]{2,1,0:T(8,128)(2,1)}, u32[]{:S(2)}, u32[]{:S(2)}) collective-permute-start(bf16[4,512,256]{2,1,0:T(8,128)(2,1)} %get-tuple-element.39), channel_id=1, source_target_pairs={{0,1},{1,2},{2,3},{3,0},{4,5},{5,6},{6,7},{7,4},{8,9},{9,10},{10,1... | collective-permute-start | bytes 3145736 | tf_op jit(solution)/shard_map/ppermute | solution.py:523
  133.1 113.0 %collective-permute-start.10 = (bf16[4,512,256]{2,1,0:T(8,128)(2,1)}, bf16[4,512,256]{2,1,0:T(8,128)(2,1)}, u32[]{:S(2)}, u32[]{:S(2)}) collective-permute-start(bf16[4,512,256]{2,1,0:T(8,128)(2,1)} %get-tuple-element.40), channel_id=1, source_target_pairs={{0,2},{1,3},{2,0},{3,1},{4,6},{5,7},{6,4},{7,5},{8,10},{9,11},{10,... | collective-permute-start | bytes 3145736 | tf_op jit(solution)/shard_map/ppermute | solution.py:523
  133.5 50.6 %collective-permute-start = (bf16[17472]{0:T(1024)(128)(2,1)S(1)}, bf16[17472]{0:T(1024)(128)(2,1)S(1)}, u32[]{:S(2)}, u32[]{:S(2)}) collective-permute-start(bf16[17472]{0:T(1024)(128)(2,1)S(1)} %concatenate.35), channel_id=1, source_target_pairs={{0,1},{1,2},{2,3},{3,0},{4,5},{5,6},{6,7},{7,4},{8,9},{9,10},{10,1... | collective-permute-start | bytes 104840 | tf_op jit(solution)/shard_map/ppermute | solution.py:523
  133.6 95.4 %collective-permute-start.1 = (bf16[17472]{0:T(1024)(128)(2,1)S(1)}, bf16[17472]{0:T(1024)(128)(2,1)S(1)}, u32[]{:S(2)}, u32[]{:S(2)}) collective-permute-start(bf16[17472]{0:T(1024)(128)(2,1)S(1)} %concatenate.35), channel_id=1, source_target_pairs={{0,2},{1,3},{2,0},{3,1},{4,6},{5,7},{6,4},{7,5},{8,10},{9,11},{10,... | collective-permute-start | bytes 104840 | tf_op jit(solution)/shard_map/ppermute | solution.py:523
  184.1 61.1 %collective-permute-start.2 = (bf16[17472]{0:T(1024)(128)(2,1)S(1)}, bf16[17472]{0:T(1024)(128)(2,1)S(1)}, u32[]{:S(2)}, u32[]{:S(2)}) collective-permute-start(bf16[17472]{0:T(1024)(128)(2,1)S(1)} %concatenate.35), channel_id=1, source_target_pairs={{0,3},{1,0},{2,1},{3,2},{4,7},{5,4},{6,5},{7,6},{8,11},{9,8},{10,9... | collective-permute-start | bytes 104840 | tf_op jit(solution)/shard_map/ppermute | solution.py:523
  229.0 100.9 %collective-permute-start.11 = (bf16[4,512,256]{2,1,0:T(8,128)(2,1)}, bf16[4,512,256]{2,1,0:T(8,128)(2,1)}, u32[]{:S(2)}, u32[]{:S(2)}) collective-permute-start(bf16[4,512,256]{2,1,0:T(8,128)(2,1)} %get-tuple-element.41), channel_id=1, source_target_pairs={{0,3},{1,0},{2,1},{3,2},{4,7},{5,4},{6,5},{7,6},{8,11},{9,8},{10,9... | collective-permute-start | bytes 3145736 | tf_op jit(solution)/shard_map/ppermute | solution.py:523
  245.1 91.5 %collective-permute-start.12 = (bf16[4,512,256]{2,1,0:T(8,128)(2,1)}, bf16[4,512,256]{2,1,0:T(8,128)(2,1)}, u32[]{:S(2)}, u32[]{:S(2)}) collective-permute-start(bf16[4,512,256]{2,1,0:T(8,128)(2,1)} %get-tuple-element.42), channel_id=1, source_target_pairs={{0,1},{1,2},{2,3},{3,0},{4,5},{5,6},{6,7},{7,4},{8,9},{9,10},{10,1... | collective-permute-start | bytes 3145736 | tf_op jit(solution)/shard_map/ppermute | solution.py:523
  245.2 161.7 %collective-permute-start.13 = (bf16[4,512,256]{2,1,0:T(8,128)(2,1)}, bf16[4,512,256]{2,1,0:T(8,128)(2,1)}, u32[]{:S(2)}, u32[]{:S(2)}) collective-permute-start(bf16[4,512,256]{2,1,0:T(8,128)(2,1)} %get-tuple-element.43), channel_id=1, source_target_pairs={{0,2},{1,3},{2,0},{3,1},{4,6},{5,7},{6,4},{7,5},{8,10},{9,11},{10,... | collective-permute-start | bytes 3145736 | tf_op jit(solution)/shard_map/ppermute | solution.py:523
  246.1 162.6 %collective-permute-start.14 = (bf16[4,512,256]{2,1,0:T(8,128)(2,1)}, bf16[4,512,256]{2,1,0:T(8,128)(2,1)}, u32[]{:S(2)}, u32[]{:S(2)}) collective-permute-start(bf16[4,512,256]{2,1,0:T(8,128)(2,1)} %get-tuple-element.44), channel_id=1, source_target_pairs={{0,3},{1,0},{2,1},{3,2},{4,7},{5,4},{6,5},{7,6},{8,11},{9,8},{10,9... | collective-permute-start | bytes 3145736 | tf_op jit(solution)/shard_map/ppermute | solution.py:523
  459.4 42.4 %collective-permute-start.15 = (bf16[192,2048]{1,0:T(8,128)(2,1)}, bf16[192,2048]{1,0:T(8,128)(2,1)S(1)}, u32[]{:S(2)}, u32[]{:S(2)}) collective-permute-start(bf16[192,2048]{1,0:T(8,128)(2,1)} %get-tuple-element.84), channel_id=1, source_target_pairs={{0,1},{1,2},{2,3},{3,0},{4,5},{5,6},{6,7},{7,4},{8,9},{9,10},{10,1... | collective-permute-start | bytes 2359304 | tf_op jit(solution)/shard_map/ppermute | solution.py:523
  480.2 54.4 %collective-permute-start.16 = (bf16[192,2048]{1,0:T(8,128)(2,1)}, bf16[192,2048]{1,0:T(8,128)(2,1)S(1)}, u32[]{:S(2)}, u32[]{:S(2)}) collective-permute-start(bf16[192,2048]{1,0:T(8,128)(2,1)} %get-tuple-element.86), channel_id=1, source_target_pairs={{0,2},{1,3},{2,0},{3,1},{4,6},{5,7},{6,4},{7,5},{8,10},{9,11},{10,... | collective-permute-start | bytes 2359304 | tf_op jit(solution)/shard_map/ppermute | solution.py:523
  483.6 51.1 %collective-permute-start.17 = (bf16[192,2048]{1,0:T(8,128)(2,1)}, bf16[192,2048]{1,0:T(8,128)(2,1)S(1)}, u32[]{:S(2)}, u32[]{:S(2)}) collective-permute-start(bf16[192,2048]{1,0:T(8,128)(2,1)} %get-tuple-element.85), channel_id=1, source_target_pairs={{0,3},{1,0},{2,1},{3,2},{4,7},{5,4},{6,5},{7,6},{8,11},{9,8},{10,9... | collective-permute-start | bytes 2359304 | tf_op jit(solution)/shard_map/ppermute | solution.py:523
  538.7 896.6 %reduce-scatter.4.cloned.1.call-start = ((), (), s32[]{:S(2)}) async-start(), calls=%async_computation.6 | async-start | bytes 3932160 | tf_op jit(solution)/shard_map/reduce_scatter | solution.py:826
  932.8 70.6 %collective-permute-start.19 = (bf16[2,768,1024]{2,1,0:T(8,128)(2,1)}, bf16[2,768,1024]{2,1,0:T(8,128)(2,1)}, u32[]{:S(2)}, u32[]{:S(2)}) collective-permute-start(bf16[2,768,1024]{2,1,0:T(8,128)(2,1)} %dynamic-slice_bitcast_fusion.4), channel_id=1, source_target_pairs={{0,8},{4,12},{8,0},{12,4},{16,24},{20,28},{24,16},{28,20},{1,9},{5... | collective-permute-start | bytes 9437192 | tf_op jit(solution)/shard_map/ppermute | solution.py:569
  938.4 79.7 %collective-permute-start.21 = (bf16[2,768,1152]{2,1,0:T(8,128)(2,1)}, bf16[2,768,1152]{2,1,0:T(8,128)(2,1)}, u32[]{:S(2)}, u32[]{:S(2)}) collective-permute-start(bf16[2,768,1152]{2,1,0:T(8,128)(2,1)} %dynamic-slice_bitcast_fusion.1), channel_id=1, source_target_pairs={{0,16},{4,20},{8,24},{12,28},{16,0},{20,4},{24,8},{28,12},{1,17},{... | collective-permute-start | bytes 10616840 | tf_op jit(solution)/shard_map/ppermute | solution.py:569
  939.0 84.6 %collective-permute-start.23 = (bf16[4,256,512]{2,1,0:T(8,128)(2,1)}, bf16[4,256,512]{2,1,0:T(8,128)(2,1)S(1)}, u32[]{:S(2)}, u32[]{:S(2)}) collective-permute-start(bf16[4,256,512]{2,1,0:T(8,128)(2,1)} %get-tuple-element.50), channel_id=1, source_target_pairs={{0,1},{1,2},{2,3},{3,0},{4,5},{5,6},{6,7},{7,4},{8,9},{9,10},{10,1... | collective-permute-start | bytes 3145736 | tf_op jit(solution)/shard_map/ppermute | solution.py:523
  939.0 84.6 %collective-permute-start.24 = (bf16[4,256,512]{2,1,0:T(8,128)(2,1)}, bf16[4,256,512]{2,1,0:T(8,128)(2,1)S(1)}, u32[]{:S(2)}, u32[]{:S(2)}) collective-permute-start(bf16[4,256,512]{2,1,0:T(8,128)(2,1)} %get-tuple-element.51), channel_id=1, source_target_pairs={{0,2},{1,3},{2,0},{3,1},{4,6},{5,7},{6,4},{7,5},{8,10},{9,11},{10,... | collective-permute-start | bytes 3145736 | tf_op jit(solution)/shard_map/ppermute | solution.py:523
  941.0 84.6 %collective-permute-start.25 = (bf16[4,256,512]{2,1,0:T(8,128)(2,1)}, bf16[4,256,512]{2,1,0:T(8,128)(2,1)S(1)}, u32[]{:S(2)}, u32[]{:S(2)}) collective-permute-start(bf16[4,256,512]{2,1,0:T(8,128)(2,1)} %get-tuple-element.52), channel_id=1, source_target_pairs={{0,3},{1,0},{2,1},{3,2},{4,7},{5,4},{6,5},{7,6},{8,11},{9,8},{10,9... | collective-permute-start | bytes 3145736 | tf_op jit(solution)/shard_map/ppermute | solution.py:523
  1009.2 115.0 %collective-permute-start.20 = (bf16[768,1024]{1,0:T(8,128)(2,1)}, bf16[768,1024]{1,0:T(8,128)(2,1)}, u32[]{:S(2)}, u32[]{:S(2)}) collective-permute-start(bf16[768,1024]{1,0:T(8,128)(2,1)} %dynamic-slice_bitcast_fusion.8), channel_id=1, source_target_pairs={{0,16},{4,20},{8,24},{12,28},{16,0},{20,4},{24,8},{28,12},{1,17},{... | collective-permute-start | bytes 4718600 | tf_op jit(solution)/shard_map/ppermute | solution.py:569
  1022.9 104.0 %collective-permute-start.22 = (bf16[768,1152]{1,0:T(8,128)(2,1)S(1)}, bf16[768,1152]{1,0:T(8,128)(2,1)}, u32[]{:S(2)}, u32[]{:S(2)}) collective-permute-start(bf16[768,1152]{1,0:T(8,128)(2,1)S(1)} %dynamic-slice_bitcast_fusion.5), channel_id=1, source_target_pairs={{0,8},{4,12},{8,0},{12,4},{16,24},{20,28},{24,16},{28,20},{1,9},{5... | collective-permute-start | bytes 5308424 | tf_op jit(solution)/shard_map/ppermute | solution.py:569
  1023.6 28.1 %collective-permute-start.26 = (bf16[4,256,512]{2,1,0:T(8,128)(2,1)}, bf16[4,256,512]{2,1,0:T(8,128)(2,1)S(1)}, u32[]{:S(2)}, u32[]{:S(2)}) collective-permute-start(bf16[4,256,512]{2,1,0:T(8,128)(2,1)} %get-tuple-element.53), channel_id=1, source_target_pairs={{0,1},{1,2},{2,3},{3,0},{4,5},{5,6},{6,7},{7,4},{8,9},{9,10},{10,1... | collective-permute-start | bytes 3145736 | tf_op jit(solution)/shard_map/ppermute | solution.py:523
  1023.6 77.3 %collective-permute-start.27 = (bf16[4,256,512]{2,1,0:T(8,128)(2,1)}, bf16[4,256,512]{2,1,0:T(8,128)(2,1)}, u32[]{:S(2)}, u32[]{:S(2)}) collective-permute-start(bf16[4,256,512]{2,1,0:T(8,128)(2,1)} %get-tuple-element.54), channel_id=1, source_target_pairs={{0,2},{1,3},{2,0},{3,1},{4,6},{5,7},{6,4},{7,5},{8,10},{9,11},{10,... | collective-permute-start | bytes 3145736 | tf_op jit(solution)/shard_map/ppermute | solution.py:523
  1025.6 96.7 %collective-permute-start.28 = (bf16[4,256,512]{2,1,0:T(8,128)(2,1)}, bf16[4,256,512]{2,1,0:T(8,128)(2,1)}, u32[]{:S(2)}, u32[]{:S(2)}) collective-permute-start(bf16[4,256,512]{2,1,0:T(8,128)(2,1)} %get-tuple-element.55), channel_id=1, source_target_pairs={{0,3},{1,0},{2,1},{3,2},{4,7},{5,4},{6,5},{7,6},{8,11},{9,8},{10,9... | collective-permute-start | bytes 3145736 | tf_op jit(solution)/shard_map/ppermute | solution.py:523
  1130.6 23.7 %collective-permute-start.29 = (bf16[192,2176]{1,0:T(8,128)(2,1)}, bf16[192,2176]{1,0:T(8,128)(2,1)}, u32[]{:S(2)}, u32[]{:S(2)}) collective-permute-start(bf16[192,2176]{1,0:T(8,128)(2,1)} %get-tuple-element.78), channel_id=1, source_target_pairs={{0,1},{1,2},{2,3},{3,0},{4,5},{5,6},{6,7},{7,4},{8,9},{9,10},{10,1... | collective-permute-start | bytes 2506760 | tf_op jit(solution)/shard_map/ppermute | solution.py:523
  1131.4 57.7 %collective-permute-start.30 = (bf16[192,2176]{1,0:T(8,128)(2,1)}, bf16[192,2176]{1,0:T(8,128)(2,1)}, u32[]{:S(2)}, u32[]{:S(2)}) collective-permute-start(bf16[192,2176]{1,0:T(8,128)(2,1)} %get-tuple-element.79), channel_id=1, source_target_pairs={{0,2},{1,3},{2,0},{3,1},{4,6},{5,7},{6,4},{7,5},{8,10},{9,11},{10,... | collective-permute-start | bytes 2506760 | tf_op jit(solution)/shard_map/ppermute | solution.py:523
  1134.6 54.5 %collective-permute-start.31 = (bf16[192,2176]{1,0:T(8,128)(2,1)}, bf16[192,2176]{1,0:T(8,128)(2,1)}, u32[]{:S(2)}, u32[]{:S(2)}) collective-permute-start(bf16[192,2176]{1,0:T(8,128)(2,1)} %get-tuple-element.80), channel_id=1, source_target_pairs={{0,3},{1,0},{2,1},{3,2},{4,7},{5,4},{6,5},{7,6},{8,11},{9,8},{10,9... | collective-permute-start | bytes 2506760 | tf_op jit(solution)/shard_map/ppermute | solution.py:523
  1242.3 70.5 %collective-permute-start.33 = (bf16[2,768,1024]{2,1,0:T(8,128)(2,1)}, bf16[2,768,1024]{2,1,0:T(8,128)(2,1)}, u32[]{:S(2)}, u32[]{:S(2)}) collective-permute-start(bf16[2,768,1024]{2,1,0:T(8,128)(2,1)} %dynamic-slice_bitcast_fusion.3), channel_id=1, source_target_pairs={{0,8},{4,12},{8,0},{12,4},{16,24},{20,28},{24,16},{28,20},{1,9},{5... | collective-permute-start | bytes 9437192 | tf_op jit(solution)/shard_map/ppermute | solution.py:569
  1247.8 71.0 %collective-permute-start.35 = (bf16[2,768,1024]{2,1,0:T(8,128)(2,1)}, bf16[2,768,1024]{2,1,0:T(8,128)(2,1)}, u32[]{:S(2)}, u32[]{:S(2)}) collective-permute-start(bf16[2,768,1024]{2,1,0:T(8,128)(2,1)} %dynamic-slice_bitcast_fusion.2), channel_id=1, source_target_pairs={{0,16},{4,20},{8,24},{12,28},{16,0},{20,4},{24,8},{28,12},{1,17},{... | collective-permute-start | bytes 9437192 | tf_op jit(solution)/shard_map/ppermute | solution.py:569
  1317.3 35.6 %collective-permute-start.34 = (bf16[768,1024]{1,0:T(8,128)(2,1)S(1)}, bf16[768,1024]{1,0:T(8,128)(2,1)S(1)}, u32[]{:S(2)}, u32[]{:S(2)}) collective-permute-start(bf16[768,1024]{1,0:T(8,128)(2,1)S(1)} %dynamic-slice_bitcast_fusion.7), channel_id=1, source_target_pairs={{0,16},{4,20},{8,24},{12,28},{16,0},{20,4},{24,8},{28,12},{1,17},{... | collective-permute-start | bytes 4718600 | tf_op jit(solution)/shard_map/ppermute | solution.py:569
  1322.4 35.4 %collective-permute-start.36 = (bf16[768,1024]{1,0:T(8,128)(2,1)S(1)}, bf16[768,1024]{1,0:T(8,128)(2,1)S(1)}, u32[]{:S(2)}, u32[]{:S(2)}) collective-permute-start(bf16[768,1024]{1,0:T(8,128)(2,1)S(1)} %dynamic-slice_bitcast_fusion.6), channel_id=1, source_target_pairs={{0,8},{4,12},{8,0},{12,4},{16,24},{20,28},{24,16},{28,20},{1,9},{5... | collective-permute-start | bytes 4718600 | tf_op jit(solution)/shard_map/ppermute | solution.py:569
  1360.5 143.0 %all-gather.11.cloned.1.call-start = ((), (), s32[]{:S(2)}) async-start(), calls=%async_computation.7 | async-start | bytes 3932160 | tf_op jit(solution)/shard_map/all_gather | solution.py:779
  1440.0 212.9 %reduce-scatter.8.cloned.1.call-start = ((), (), s32[]{:S(2)}) async-start(), calls=%async_computation.9 | async-start | bytes 2359296 | tf_op jit(solution)/shard_map/reduce_scatter | solution.py:793
  1508.7 145.8 %reduce-scatter.6.cloned.1.call-start = ((), (), s32[]{:S(2)}) async-start(), calls=%async_computation.8 | async-start | bytes 7077888 | tf_op jit(solution)/shard_map/reduce_scatter | solution.py:799
  1570.5 34.2 %collective-permute-start.37 = (bf16[192,2048]{1,0:T(8,128)(2,1)}, bf16[192,2048]{1,0:T(8,128)(2,1)S(1)}, u32[]{:S(2)}, u32[]{:S(2)}) collective-permute-start(bf16[192,2048]{1,0:T(8,128)(2,1)} %get-tuple-element.81), channel_id=1, source_target_pairs={{0,1},{1,2},{2,3},{3,0},{4,5},{5,6},{6,7},{7,4},{8,9},{9,10},{10,1... | collective-permute-start | bytes 2359304 | tf_op jit(solution)/shard_map/ppermute | solution.py:523
  1570.5 55.4 %collective-permute-start.38 = (bf16[192,2048]{1,0:T(8,128)(2,1)}, bf16[192,2048]{1,0:T(8,128)(2,1)}, u32[]{:S(2)}, u32[]{:S(2)}) collective-permute-start(bf16[192,2048]{1,0:T(8,128)(2,1)} %get-tuple-element.83), channel_id=1, source_target_pairs={{0,2},{1,3},{2,0},{3,1},{4,6},{5,7},{6,4},{7,5},{8,10},{9,11},{10,... | collective-permute-start | bytes 2359304 | tf_op jit(solution)/shard_map/ppermute | solution.py:523
  1571.8 54.1 %collective-permute-start.39 = (bf16[192,2048]{1,0:T(8,128)(2,1)}, bf16[192,2048]{1,0:T(8,128)(2,1)}, u32[]{:S(2)}, u32[]{:S(2)}) collective-permute-start(bf16[192,2048]{1,0:T(8,128)(2,1)} %get-tuple-element.82), channel_id=1, source_target_pairs={{0,3},{1,0},{2,1},{3,2},{4,7},{5,4},{6,5},{7,6},{8,11},{9,8},{10,9... | collective-permute-start | bytes 2359304 | tf_op jit(solution)/shard_map/ppermute | solution.py:523
  1576.9 24.2 %collective-permute-start.41 = (f32[2,256,128]{2,1,0:T(8,128)S(1)}, f32[2,256,128]{2,1,0:T(8,128)}, u32[]{:S(2)}, u32[]{:S(2)}) collective-permute-start(f32[2,256,128]{2,1,0:T(8,128)S(1)} %dynamic-slice_bitcast_fusion.9), channel_id=1, source_target_pairs={{0,16},{4,20},{8,24},{12,28},{16,0},{20,4},{24,8},{28,12},{1,17},{... | collective-permute-start | bytes 786440 | tf_op jit(solution)/shard_map/ppermute | solution.py:569
  1603.1 25.2 %collective-permute-start.42 = (f32[256,128]{0,1:T(8,128)}, f32[256,128]{0,1:T(8,128)S(1)}, u32[]{:S(2)}, u32[]{:S(2)}) collective-permute-start(f32[256,128]{0,1:T(8,128)} %bitcast.233), channel_id=1, source_target_pairs={{0,8},{4,12},{8,0},{12,4},{16,24},{20,28},{24,16},{28,20},{1,9},{5... | collective-permute-start | bytes 393224 | tf_op jit(solution)/shard_map/ppermute | solution.py:569
  1628.5 22.7 %collective-permute-start.43 = (f32[64,128]{0,1:T(8,128)S(1)}, f32[64,128]{0,1:T(8,128)S(1)}, u32[]{:S(2)}, u32[]{:S(2)}) collective-permute-start(f32[64,128]{0,1:T(8,128)S(1)} %get-tuple-element.111), channel_id=1, source_target_pairs={{0,1},{1,2},{2,3},{3,0},{4,5},{5,6},{6,7},{7,4},{8,9},{9,10},{10,1... | collective-permute-start | bytes 98312 | tf_op jit(solution)/shard_map/ppermute | solution.py:523
  1655.9 24.0 %collective-permute-start.46 = (bf16[64,1536]{1,0:T(8,128)(2,1)S(1)}, bf16[64,1536]{1,0:T(8,128)(2,1)S(1)}, u32[]{:S(2)}, u32[]{:S(2)}) collective-permute-start(bf16[64,1536]{1,0:T(8,128)(2,1)S(1)} %get-tuple-element.99), channel_id=1, source_target_pairs={{0,1},{1,2},{2,3},{3,0},{4,5},{5,6},{6,7},{7,4},{8,9},{9,10},{10,1... | collective-permute-start | bytes 589832 | tf_op jit(solution)/shard_map/ppermute | solution.py:523
  1660.6 25.1 %collective-permute-start.47 = (bf16[64,1536]{1,0:T(8,128)(2,1)S(1)}, bf16[64,1536]{1,0:T(8,128)(2,1)S(1)}, u32[]{:S(2)}, u32[]{:S(2)}) collective-permute-start(bf16[64,1536]{1,0:T(8,128)(2,1)S(1)} %get-tuple-element.98), channel_id=1, source_target_pairs={{0,2},{1,3},{2,0},{3,1},{4,6},{5,7},{6,4},{7,5},{8,10},{9,11},{10,... | collective-permute-start | bytes 589832 | tf_op jit(solution)/shard_map/ppermute | solution.py:523
  (76 other events, 2711.6 us)
Sparse Core Ops, SparseCore 0:
  9.6 80.6 all-gather.4
  93.0 307.8 all-gather.8
  538.8 169.2 all-gather.6
  1360.6 74.6 reduce-scatter.3
  1440.1 63.3 all-gather.10
  1508.8 39.7 reduce-scatter.7
  1552.0 66.6 reduce-scatter.5
